TPU v7x, 32 devices: a whole 2x2x4 slice. The times are simulated.
32 devices in a mesh: tile: 8 (over y, x, core), lev: 4 (over z).
Axes of the slice: x: 2, y: 2, z: 4, core: 2. Of those that a mesh axis runs over, the one named last changes fastest.
Arguments:
- members_pert: bfloat16 [64, 16, 32768], P('lev', None, 'tile'), may hold values from -4 to 4
- coarse_pert: bfloat16 [64, 8, 2048], P('lev', None, 'tile'), may hold values from -6 to 6
- member_ctrl: bfloat16 [64, 16, 2048], P('lev', None, 'tile'), may hold values from -6 to 6
- coarse_ctrl: bfloat16 [64, 8, 2048], P('lev', None, 'tile'), may hold values from -6 to 6
- vert_loc: float32 [64, 64], replicated, may hold values from -1.5 to 1.5, as said below
- stencil: int32 [4, 32768], P(None, 'tile'), may hold values from 0 to 383, as said below
- interp_w: bfloat16 [4, 32768], P(None, 'tile'), may hold values from 0 to 1, as said below
Outputs:
- member_out: float32 [64, 16, 2048], P('lev', None, 'tile')
- coarse_out: float32 [64, 8, 2048], P('lev', None, 'tile')
Inputs may be any that keep to these rules, and one draw needn't show every extreme that they name: vert_loc[i, j] is zero where |i - j| > 4, and nonzero where |i - j| = 4. stencil indexes a window of 384 coarse cells of the fine cell's tile index: the last 64 coarse cells of the tile index before it (the first one's predecessor is the last), its own 256 cells, then the first 64 cells of the tile index after it; the four corners of a fine cell are distinct. `interp_w`: the four weights of a fine cell are nonnegative and sum to one up to rounding.
All inputs are finite; a program needn't handle non-finite values.
Results may differ from a plain program's by a relative error of at most 0.013.
Values may be sent and summed in bfloat16 or wider, within the bound.
A program may use at most 64 MiB of HBM per device.

v0:
```python
import functools

import jax
import jax.numpy as jnp
from jax import lax
from jax.experimental import pallas as pl
from jax.experimental.pallas import tpu as pltpu
from jax.sharding import PartitionSpec as P

HB = 4
CW = 64
LANE = 128
CHUNK = 1024
MESH = pl.DeviceIdType.MESH
F32 = jnp.float32
BF16 = jnp.bfloat16

DIRECTIONS = ((0, -1), (0, 1), (-1, 0), (1, 0), (-1, -1), (1, -1), (-1, 1), (1, 1))


def kernel(
    tiles, levs, pert_hbm, cp_hbm, mc_hbm, cc_hbm, vert_hbm, st_hbm, w_hbm, mo, co,
    mc, cc, cp, pert, vert, st, w, matrix, fld, comb, adj, inc, acc, out_buf, r_tile, r_lev, r_diag,
    load_sem, send1, recv1, send2, recv2,
):
    rows, members, cells = mc_hbm.shape
    group = cc_hbm.shape[1]
    total_levels = vert_hbm.shape[0]
    fine = pert_hbm.shape[2]
    span = cells + LANE
    edge = HB * members + rows
    comb_at = (rows - HB) * members
    tail_at = comb_at - HB * members

    def level_at(i):
        return (i - HB) * members if i >= HB else comb_at + rows + i * members

    t = lax.axis_index("tile")
    v = lax.axis_index("lev")
    first = v * rows
    has = {-1: v > 0, 0: None, 1: v < levs - 1}

    def when(dl, action):
        if dl == 0:
            action()
        else:
            pl.when(has[dl])(action)

    def device(dt, dl):
        return (lax.rem(t + dt + tiles, tiles), lax.rem(v + dl + levs, levs))

    own = pl.ds(HB, rows)
    loads = [
        pltpu.make_async_copy(mc_hbm, mc.at[own, :, pl.ds(0, cells)], load_sem.at[0]),
        pltpu.make_async_copy(cc_hbm, cc.at[own, :, pl.ds(0, cells)], load_sem.at[1]),
        pltpu.make_async_copy(cp_hbm, cp.at[own, :, pl.ds(0, cells)], load_sem.at[2]),
        pltpu.make_async_copy(st_hbm, st, load_sem.at[3]),
        pltpu.make_async_copy(w_hbm, w, load_sem.at[4]),
        pltpu.make_async_copy(vert_hbm, vert, load_sem.at[5]),
        pltpu.make_async_copy(pert_hbm, pert, load_sem.at[6]),
    ]
    for load in loads:
        load.start()

    barrier = pltpu.get_barrier_semaphore()
    for dt, dl in DIRECTIONS:
        when(
            dl,
            lambda dt=dt, dl=dl: pl.semaphore_signal(
                barrier, inc=1, device_id=device(dt, dl), device_id_type=MESH
            ),
        )

    level_src = {0: (HB, rows), 1: (rows, HB), -1: (HB, HB)}
    level_dst = {0: HB, 1: 0, -1: HB + rows}
    lane_src = {0: (0, cells), 1: (cells - LANE, LANE), -1: (0, LANE)}
    lane_dst = {0: 0, 1: cells + LANE, -1: cells}
    wanted = [(buf, direction) for direction in DIRECTIONS for buf in (mc, cc)]
    wanted += [(cp, direction) for direction in ((-1, 0), (1, 0), (0, -1), (0, 1))]
    round1 = []
    for n, (buf, (dt, dl)) in enumerate(wanted):
        (l0, ln), (c0, cn) = level_src[dl], lane_src[dt]
        copy = pltpu.make_async_remote_copy(
            src_ref=buf.at[pl.ds(l0, ln), :, pl.ds(c0, cn)],
            dst_ref=buf.at[pl.ds(level_dst[dl], ln), :, pl.ds(lane_dst[dt], cn)],
            send_sem=send1.at[n],
            recv_sem=recv1.at[n],
            device_id=device(dt, dl),
            device_id_type=MESH,
        )
        round1.append((dl, copy))
    needed = {"own": round1[:4], "rim": round1[4:-2], "spread": round1[-2:]}

    def arrive(stage):
        for dl, copy in needed[stage]:
            when(-dl, copy.wait_recv)

    @pl.when(v == 0)
    def _():
        for buf in (mc, cc, cp):
            buf[0:HB] = jnp.zeros((HB,) + buf.shape[1:], BF16)
        r_lev[0] = jnp.zeros(r_lev.shape[1:], BF16)
        r_diag[0] = jnp.zeros(r_diag.shape[1:], BF16)

    @pl.when(v == levs - 1)
    def _():
        for buf in (mc, cc, cp):
            buf[HB + rows :] = jnp.zeros((HB,) + buf.shape[1:], BF16)
        r_lev[1] = jnp.zeros(r_lev.shape[1:], BF16)
        r_diag[1] = jnp.zeros(r_diag.shape[1:], BF16)

    for load in loads[:3]:
        load.wait()
    neighbours = 2 + 3 * jnp.where(v > 0, 1, 0) + 3 * jnp.where(v < levs - 1, 1, 0)
    pl.semaphore_wait(barrier, neighbours)
    for dl, copy in round1:
        when(dl, copy.start)

    for load in loads[3:6]:
        load.wait()
    pack = 16
    base_rows = lax.broadcasted_iota(jnp.int32, (pack, LANE), 0).astype(jnp.int16)

    def build(step, carry):
        lanes = pl.ds(pl.multiple_of(step * LANE, LANE), LANE)
        places, weights = [], []
        for corner in range(4):
            cell = st[corner : corner + 1, lanes] - CW
            cell = jnp.where(cell < 0, cell + span, cell)
            places.append(jnp.broadcast_to(cell, (pack, LANE)).astype(jnp.int16))
            weight = w[corner : corner + 1, lanes].astype(F32)
            weights.append(jnp.broadcast_to(weight, (pack, LANE)).astype(BF16))
        for block in range(span // pack):
            index = base_rows + jnp.int16(block * pack)
            value = jnp.zeros((pack, LANE), BF16)
            for corner in range(4):
                value = jnp.where(places[corner] == index, weights[corner], value)
            matrix[block * pack : (block + 1) * pack, lanes] = value
        return carry

    lax.fori_loop(0, fine // LANE, build, 0)

    next_side = lax.broadcasted_iota(jnp.int32, (1, LANE), 1) < LANE - CW

    def window(buf, level, lane_tile):
        if lane_tile * LANE < cells:
            return buf[level, :, lane_tile * LANE : (lane_tile + 1) * LANE].astype(F32)
        from_next = buf[level, :, cells : cells + LANE].astype(F32)
        from_prev = buf[level, :, cells + LANE : cells + 2 * LANE].astype(F32)
        return jnp.where(next_side, from_next, from_prev)

    def factor(i, j):
        return vert[
            lax.rem(first + i + total_levels, total_levels),
            lax.rem(first + j + total_levels, total_levels),
        ]

    for lane_tile in range(span // LANE):
        if lane_tile == 0:
            arrive("own")
        if lane_tile * LANE == cells:
            arrive("rim")
        lanes = slice(lane_tile * LANE, (lane_tile + 1) * LANE)
        values = [window(mc, level, lane_tile) for level in range(rows + 2 * HB)]
        for i in range(rows):
            total = factor(i, i - HB) * values[i]
            for d in range(1, 2 * HB + 1):
                total = total + factor(i, i + d - HB) * values[i + d]
            at = level_at(i)
            fld[at : at + members, lanes] = total.astype(BF16)
        values = [window(cc, level, lane_tile) for level in range(rows + 2 * HB)]
        for i in range(rows):
            total = factor(i, i - HB) * values[i]
            for d in range(1, 2 * HB + 1):
                total = total + factor(i, i + d - HB) * values[i + d]
            total = total.astype(BF16).astype(F32) * window(cp, i + HB, lane_tile)
            comb[i : i + 1, lanes] = jnp.sum(total, axis=0, keepdims=True)
    fld[comb_at : comb_at + rows, :] = comb[...].astype(BF16)

    loads[6].wait()
    for chunk in range(fine // CHUNK):
        lanes = slice(chunk * CHUNK, (chunk + 1) * CHUNK)
        interp = jnp.dot(fld[...], matrix[:, lanes], preferred_element_type=F32)
        for i in range(rows):
            at = level_at(i)
            member = pert[i, :, lanes].astype(F32)
            line = jnp.sum(member * interp[at : at + members], axis=0, keepdims=True)
            line = line + interp[comb_at + i : comb_at + i + 1]
            adj[at : at + members, lanes] = (member * line).astype(BF16)
            inc[i : i + 1, lanes] = line
        adj[comb_at : comb_at + rows, lanes] = inc[:, lanes].astype(BF16)
        back = lax.dot_general(
            adj[:, lanes], matrix[:, lanes], (((1,), (1,)), ((), ())), preferred_element_type=F32
        )
        if chunk == 0:
            acc[...] = back
        else:
            acc[...] += back
    out_buf[...] = acc[...].astype(BF16)

    row_src = {0: (0, acc.shape[0]), 1: (tail_at, edge), -1: (comb_at, edge)}
    round2 = []
    for n, (dt, dl) in enumerate(DIRECTIONS):
        r0, rn = row_src[dl]
        side, floor = (1 - dt) // 2, (1 - dl) // 2
        if dt == 0:
            src, dst = out_buf.at[pl.ds(r0, rn), pl.ds(0, cells)], r_lev.at[floor]
        else:
            src = out_buf.at[pl.ds(r0, rn), pl.ds(cells, LANE)]
            dst = r_tile.at[side] if dl == 0 else r_diag.at[floor, side]
        copy = pltpu.make_async_remote_copy(
            src_ref=src,
            dst_ref=dst,
            send_sem=send2.at[n],
            recv_sem=recv2.at[n],
            device_id=device(dt, dl),
            device_id_type=MESH,
        )
        round2.append((dl, copy))
    for dl, copy in round2:
        when(dl, copy.start)
    arrive("spread")
    for dl, copy in round2:
        when(-dl, copy.wait_recv)

    tile_lanes = lax.broadcasted_iota(jnp.int32, (1, LANE), 1)
    for lane_tile in range(cells // LANE):
        lanes = slice(lane_tile * LANE, (lane_tile + 1) * LANE)

        def joined(base, prev, following):
            if lane_tile == 0:
                base = base + jnp.where(tile_lanes < CW, prev.astype(F32), 0.0)
            if lane_tile == cells // LANE - 1:
                base = base + jnp.where(tile_lanes >= LANE - CW, following.astype(F32), 0.0)
            return base

        def halo(floor, r0, rn):
            at = slice(r0, r0 + rn)
            return joined(
                r_lev[floor, at, lanes].astype(F32), r_diag[floor, 0, at, :], r_diag[floor, 1, at, :]
            )

        def inner(r0, rn):
            at = slice(r0, r0 + rn)
            return joined(acc[at, lanes], r_tile[0, at, :], r_tile[1, at, :])

        values = [halo(0, i * members, members) for i in range(HB)]
        values += [inner(level_at(i), members) for i in range(rows)]
        values += [halo(1, rows + i * members, members) for i in range(HB)]
        for j in range(rows):
            total = factor(j - HB, j) * values[j]
            for d in range(1, 2 * HB + 1):
                total = total + factor(j + d - HB, j) * values[j + d]
            mo[j, :, lanes] = total
        below = halo(0, HB * members, rows)
        middle = inner(comb_at, rows)
        above = halo(1, 0, rows)
        lines = [below[rows - HB + i : rows - HB + i + 1] for i in range(HB)]
        lines += [middle[i : i + 1] for i in range(rows)]
        lines += [above[i : i + 1] for i in range(HB)]
        values = [
            cp[level, :, lanes].astype(F32) * lines[level] for level in range(rows + 2 * HB)
        ]
        for j in range(rows):
            total = factor(j - HB, j) * values[j]
            for d in range(1, 2 * HB + 1):
                total = total + factor(j + d - HB, j) * values[j + d]
            co[j, :, lanes] = total

    for dl, copy in round1 + round2:
        when(dl, copy.wait_send)


def store(mo, co, mo_hbm, co_hbm, sem):
    copies = [
        pltpu.make_async_copy(mo, mo_hbm, sem.at[0]),
        pltpu.make_async_copy(co, co_hbm, sem.at[1]),
    ]
    for copy in copies:
        copy.start()
    for copy in copies:
        copy.wait()


def solution(mesh):
    tiles, levs = mesh.shape["tile"], mesh.shape["lev"]

    def step(members_pert, coarse_pert, member_ctrl, coarse_ctrl, vert_loc, stencil, interp_w):
        rows, members, cells = member_ctrl.shape
        group = coarse_ctrl.shape[1]
        fine = members_pert.shape[2]
        levels, span, lines = rows + 2 * HB, cells + LANE, rows * (members + 1)
        edge = HB * members + rows
        hbm = pl.BlockSpec(memory_space=pl.ANY)
        copies = 8 * 2 + 4
        vmem = pl.BlockSpec(memory_space=pltpu.VMEM)
        results = pl.pallas_call(
            functools.partial(kernel, tiles, levs),
            out_shape=(
                pltpu.VMEM((rows, members, cells), F32),
                pltpu.VMEM((rows, group, cells), F32),
            ),
            in_specs=[hbm] * 7,
            out_specs=(vmem, vmem),
            scratch_shapes=[
                pltpu.VMEM((levels, members, cells + 2 * LANE), BF16),
                pltpu.VMEM((levels, group, cells + 2 * LANE), BF16),
                pltpu.VMEM((levels, group, cells + 2 * LANE), BF16),
                pltpu.VMEM((rows, members, fine), BF16),
                pltpu.SMEM(vert_loc.shape, F32),
                pltpu.VMEM(stencil.shape, jnp.int32),
                pltpu.VMEM(interp_w.shape, BF16),
                pltpu.VMEM((span, fine), BF16),
                pltpu.VMEM((lines, span), BF16),
                pltpu.VMEM((rows, span), F32),
                pltpu.VMEM((lines, fine), BF16),
                pltpu.VMEM((rows, fine), F32),
                pltpu.VMEM((lines, span), F32),
                pltpu.VMEM((lines, span), BF16),
                pltpu.VMEM((2, lines, LANE), BF16),
                pltpu.VMEM((2, edge, cells), BF16),
                pltpu.VMEM((2, 2, edge, LANE), BF16),
                pltpu.SemaphoreType.DMA((7,)),
                pltpu.SemaphoreType.DMA((copies,)),
                pltpu.SemaphoreType.DMA((copies,)),
                pltpu.SemaphoreType.DMA((8,)),
                pltpu.SemaphoreType.DMA((8,)),
            ],
            compiler_params=pltpu.CompilerParams(
                collective_id=0, has_side_effects=True, vmem_limit_bytes=60 * 1024 * 1024
            ),
        )(members_pert, coarse_pert, member_ctrl, coarse_ctrl, vert_loc, stencil, interp_w)
        return pl.pallas_call(
            store,
            out_shape=(
                jax.ShapeDtypeStruct((rows, members, cells), F32),
                jax.ShapeDtypeStruct((rows, group, cells), F32),
            ),
            in_specs=[vmem, vmem],
            out_specs=(hbm, hbm),
            scratch_shapes=[pltpu.SemaphoreType.DMA((2,))],
            compiler_params=pltpu.CompilerParams(vmem_limit_bytes=1024 * 1024),
        )(*results)

    in_specs = (
        P("lev", None, "tile"),
        P("lev", None, "tile"),
        P("lev", None, "tile"),
        P("lev", None, "tile"),
        P(),
        P(None, "tile"),
        P(None, "tile"),
    )
    out_specs = (P("lev", None, "tile"), P("lev", None, "tile"))
    return jax.shard_map(step, mesh=mesh, in_specs=in_specs, out_specs=out_specs, check_vma=False)
```

profile of v0, /device:TPU:0, one launch (start us, length us, event | category | flops | bytes accessed | tf_op | source)
XLA Modules:
  0.0 20.3 jit_solution(8155824045106535355)
XLA Ops:
  0.6 18.9 %shard_map.86 = (f32[16,16,256]{2,1,0:T(8,128)S(1)}, f32[16,8,256]{2,1,0:T(8,128)S(1)}) custom-call(bf16[16,16,4096]{2,1,0:T(8,128)(2,1)} %pert_hbm.1, bf16[16,8,256]{2,1,0:T(8,128)(2,1)} %cp_hbm.1, bf16[16,16,256]{2,1,0:T(8,128)(2,1)} %mc_hbm.1, bf16[16,8,256]{2,1,0:T(8,128)(2,1)} %cc_hbm.1, f32[64,64]{1,0:T(8,128)} %vert_hbm.1, s32[4,4096]{1,0:T(4,128)} %st_hbm.1, ...), custom_call_target="tpu_custom_call" | custom-call | tf_op jit(solution)/shard_map/pallas_call | solution.py:297
  19.6 0.8 %shard_map.87 = (f32[16,16,256]{2,1,0:T(8,128)}, f32[16,8,256]{2,1,0:T(8,128)}) custom-call(f32[16,16,256]{2,1,0:T(8,128)S(1)} %get-tuple-element.4.mo, f32[16,8,256]{2,1,0:T(8,128)S(1)} %get-tuple-element.5.co), custom_call_target="tpu_custom_call" | custom-call | tf_op jit(solution)/shard_map/pallas_call | solution.py:333
where the time goes:
time: 20.5 us; the launch traced here: 20.3 us
  Pallas kernels  19.7 us (96%)
  between operations  0.64 us (3%)
    pallas_call x1, Pallas kernels, step(): pl.pallas_call(functools.partial(kernel, tiles, levs), out_shape=(pltpu.V...  18.9 us
    pallas_call x1, Pallas kernels, step(): pl.pallas_call(store, out_shape=(jax.ShapeDtypeStruct((rows, members, cel...  0.76 us

commit v1 on v0

v1 whole, which is shorter than its diff:
```python
import functools

import jax
import jax.numpy as jnp
from jax import lax
from jax.experimental import pallas as pl
from jax.experimental.pallas import tpu as pltpu
from jax.sharding import PartitionSpec as P

HB = 4
CW = 64
LANE = 128
WIDE = 8
DEEP = 8
MESH = pl.DeviceIdType.MESH
F32 = jnp.float32
BF16 = jnp.bfloat16

DIRECTIONS = ((0, -1), (0, 1), (-1, 0), (1, 0), (-1, -1), (1, -1), (-1, 1), (1, 1))


def pairs_of(rows):
    half = HB // 2
    return [(b + k, b + k + half) for b in range(0, rows, HB) for k in range(half)]


def dims(rows, members, group, cells):
    comb_at = (rows - HB) * members
    packed = comb_at // 2 + rows + HB * members // 2
    return comb_at, packed


def fold(values):
    row = lax.broadcasted_iota(jnp.int32, (8, LANE), 0)
    for stride in (1, 2, 4):
        even = (row // stride) % 2 == 0
        values = [
            jnp.where(even, a, b) + pltpu.roll(jnp.where(even, b, a), stride, 0)
            for a, b in zip(values[0::2], values[1::2])
        ]
    return values[0]


def kernel(
    tiles, levs, pert_hbm, cp_hbm, mc_hbm, cc_hbm, vert_hbm, st_hbm, w_hbm, xm, xc, bm, bc,
    mc, cc, cp, pert, vert, st, w, matrix, am, ac, rim_m, rim_c, rim_p, pk, rt, rd,
    fld, fld_rim, adj, line, acc_rim, out_own, out_rim, acc_own, r_tile, r_lev, r_diag,
    load_sem, send, recv1, recv2,
):
    rows, members, cells = mc_hbm.shape
    group = cc_hbm.shape[1]
    total_levels = vert_hbm.shape[0]
    fine = pert_hbm.shape[2]
    span = cells + LANE
    window = rows + 2 * HB
    edge = HB * members + rows
    last = cells - LANE
    comb_at, packed = dims(rows, members, group, cells)
    pcomb_at = comb_at // 2
    low_at = comb_at + rows
    tail_at = comb_at - HB * members
    ptail_at = pcomb_at - HB * members // 2
    pedge = HB * members // 2 + rows
    pairs = pairs_of(rows)
    half = HB // 2
    kinds = members + 2 * group

    def level_at(i):
        return (i - HB) * members if i >= HB else low_at + i * members

    t = lax.axis_index("tile")
    v = lax.axis_index("lev")
    first = v * rows
    has = {-1: v > 0, 0: None, 1: v < levs - 1}
    beside = {-1: jnp.where(t == 0, tiles - 1, t - 1), 0: t, 1: jnp.where(t == tiles - 1, 0, t + 1)}

    def when(dl, action):
        if dl == 0:
            action()
        else:
            pl.when(has[dl])(action)

    def begin(copies):
        for dl, copy in copies:
            when(dl, copy.start)

    def settle(ref, sem):
        pltpu.make_async_copy(ref, ref, sem).wait()

    def filler(count):
        return pert.at[0, :, pl.ds(0, count // members)]

    def drain(ref, count):
        settle(ref, send.at[0])
        when(1, lambda: settle(filler(count), send.at[1]))
        when(-1, lambda: settle(filler(count), send.at[2]))

    own = pl.ds(HB, rows)
    loads = [
        pltpu.make_async_copy(mc_hbm, mc.at[own], load_sem.at[0]),
        pltpu.make_async_copy(cc_hbm, cc.at[own], load_sem.at[1]),
        pltpu.make_async_copy(cp_hbm, cp.at[own], load_sem.at[2]),
        pltpu.make_async_copy(st_hbm, st, load_sem.at[3]),
        pltpu.make_async_copy(w_hbm, w, load_sem.at[4]),
        pltpu.make_async_copy(vert_hbm, vert, load_sem.at[5]),
        pltpu.make_async_copy(pert_hbm, pert, load_sem.at[6]),
    ]
    for load in loads[:3]:
        load.start()

    barrier = pltpu.get_barrier_semaphore()
    for dt, dl in DIRECTIONS:
        when(
            dl,
            lambda dt=dt, dl=dl: pl.semaphore_signal(
                barrier, inc=1, device_id=(beside[dt], v + dl), device_id_type=MESH
            ),
        )
    for load in loads[3:]:
        load.start()

    def remote(src, dst, send_at, recv_at, dt, dl):
        return dl, pltpu.make_async_remote_copy(
            src_ref=src, dst_ref=dst, send_sem=send_at, recv_sem=recv_at,
            device_id=(beside[dt], v + dl), device_id_type=MESH,
        )

    level_src = {1: rows, -1: HB}
    level_dst = {1: 0, -1: HB + rows}
    entry_src = {1: len(pairs) - half, -1: 0}
    tile_row = {1: ptail_at, -1: pcomb_at}
    lev_row = {1: tail_at, -1: comb_at}
    lev1, late, tile1, diag1, tile2, diag2, lev2 = [], [], [], [], [], [], []
    for dl in (-1, 1):
        floor = (1 - dl) // 2
        for buf, copies, at in ((mc, lev1, 0), (cc, lev1, 0), (cp, late, 5)):
            copies.append(remote(
                buf.at[pl.ds(level_src[dl], HB)], buf.at[pl.ds(level_dst[dl], HB)],
                send.at[1 + floor], recv1.at[at + floor], 0, dl))
        lev2.append(remote(
            out_own.at[pl.ds(lev_row[dl], edge)], r_lev.at[floor],
            send.at[1 + floor], recv2.at[floor], 0, dl))
        for dt in (-1, 1):
            side = (1 + dt) // 2
            diag1.append(remote(
                pk.at[side, pl.ds(entry_src[dl], half)], rd.at[floor, side],
                send.at[1 + floor], recv1.at[2 + floor], dt, dl))
            diag2.append(remote(
                out_rim.at[side, pl.ds(tile_row[dl], pedge)], r_diag.at[floor, side],
                send.at[1 + floor], recv2.at[2 + floor], dt, dl))
    for dt in (-1, 1):
        side = (1 + dt) // 2
        tile1.append(remote(pk.at[side], rt.at[side], send.at[0], recv1.at[4], dt, 0))
        tile2.append(remote(out_rim.at[side], r_tile.at[side], send.at[0], recv2.at[4], dt, 0))
    near = HB * (members + group) * cells
    extra = HB * group * cells

    @pl.when(v == 0)
    def _():
        for buf in (mc, cc, cp):
            buf[0:HB] = jnp.zeros((HB,) + buf.shape[1:], BF16)
        rd[0] = jnp.zeros(rd.shape[1:], BF16)
        r_lev[0] = jnp.zeros(r_lev.shape[1:], BF16)
        r_diag[0] = jnp.zeros(r_diag.shape[1:], BF16)

    @pl.when(v == levs - 1)
    def _():
        for buf in (mc, cc, cp):
            buf[HB + rows :] = jnp.zeros((HB,) + buf.shape[1:], BF16)
        rd[1] = jnp.zeros(rd.shape[1:], BF16)
        r_lev[1] = jnp.zeros(r_lev.shape[1:], BF16)
        r_diag[1] = jnp.zeros(r_diag.shape[1:], BF16)

    def lower(shape):
        return lax.broadcasted_iota(jnp.int32, shape, len(shape) - 1) < CW

    def turned(value):
        return pltpu.roll(value, CW, 1)

    for load in loads[:3]:
        load.wait()
    neighbours = 2 + 3 * jnp.where(v > 0, 1, 0) + 3 * jnp.where(v < levs - 1, 1, 0)
    pl.semaphore_wait(barrier, neighbours)
    begin(lev1)
    for k, (a, b) in enumerate(pairs):
        for buf, r0, rn in ((mc, 0, members), (cc, members, group), (cp, members + group, group)):
            low = lower((rn, LANE))
            near_a, near_b = (buf[HB + i, :, 0:LANE].astype(F32) for i in (a, b))
            far_a, far_b = (buf[HB + i, :, last:].astype(F32) for i in (a, b))
            pk[0, k, r0 : r0 + rn, :] = jnp.where(low, near_a, turned(near_b)).astype(BF16)
            pk[1, k, r0 : r0 + rn, :] = jnp.where(low, turned(far_b), far_a).astype(BF16)
    begin(diag1 + tile1)
    for load in loads[3:6]:
        load.wait()
    pack = 16
    base_rows = lax.broadcasted_iota(jnp.int32, (pack, LANE), 0).astype(jnp.int16)

    def build(step, carry):
        lanes = pl.ds(pl.multiple_of(step * LANE, LANE), LANE)
        places, weights = [], []
        for corner in range(4):
            cell = st[corner : corner + 1, lanes] - CW
            cell = jnp.where(cell < 0, cell + span, cell)
            places.append(jnp.broadcast_to(cell, (pack, LANE)).astype(jnp.int16))
            weight = w[corner : corner + 1, lanes].astype(F32)
            weights.append(jnp.broadcast_to(weight, (pack, LANE)).astype(BF16))
        for block in range(span // pack):
            index = base_rows + jnp.int16(block * pack)
            value = jnp.zeros((pack, LANE), BF16)
            for corner in range(4):
                value = jnp.where(places[corner] == index, weights[corner], value)
            matrix[step, block * pack : (block + 1) * pack, :] = value
        return carry

    lax.fori_loop(0, fine // LANE, build, 0)

    factors = vert[...].astype(BF16)
    level_k = lax.broadcasted_iota(jnp.int32, (rows, total_levels), 1)
    level_i = lax.broadcasted_iota(jnp.int32, (rows, total_levels), 0)
    pick = jnp.where(level_k == first + level_i, 1.0, 0.0).astype(BF16)
    forward = jnp.dot(pick, factors, preferred_element_type=F32).astype(BF16)
    backward = lax.dot_general(
        pick, factors, (((1,), (1,)), ((), ())), preferred_element_type=F32
    ).astype(BF16)

    def spread_out(source, height, offset):
        wide = window * height
        lane = lax.broadcasted_iota(jnp.int32, (total_levels, wide), 1) // height
        row = lax.broadcasted_iota(jnp.int32, (total_levels, wide), 0)
        chosen = jnp.where(row == first + offset(lane), 1.0, 0.0).astype(BF16)
        lines = jnp.dot(source, chosen, preferred_element_type=F32)
        at = lax.broadcasted_iota(jnp.int32, (height, wide), 1) % height
        mask = at == lax.broadcasted_iota(jnp.int32, (height, wide), 0)
        return [jnp.where(mask, lines[i : i + 1], 0.0) for i in range(rows)]

    def natural(seg):
        return seg - HB

    def stored(seg):
        return jnp.where(
            seg < HB, seg - HB,
            jnp.where(seg < rows, seg, jnp.where(seg < rows + HB, seg - rows, seg - HB)),
        )

    order = list(range(HB, rows)) + list(range(HB))
    blocks = spread_out(forward, members, natural)
    for place, i in enumerate(order):
        am[place * members : (place + 1) * members, :] = blocks[i].astype(BF16)
    blocks = spread_out(backward, members, stored)
    for i in range(rows):
        bm[i * members : (i + 1) * members, :] = blocks[i].astype(BF16)
    for out, source in ((ac, forward), (bc, backward)):
        blocks = spread_out(source, group, natural)
        for i in range(0, rows, 2):
            both = jnp.concatenate(blocks[i : i + 2], axis=0)
            out[i * group : (i + 2) * group, :] = both.astype(BF16)

    def localize(members_in, coarse_in, coarse_by, out):
        wide = members_in.shape[-1]
        value = jnp.dot(
            am[...], members_in.reshape(window * members, wide), preferred_element_type=F32
        ).astype(BF16)
        out[0:comb_at, :] = value[0:comb_at]
        out[low_at:, :] = value[comb_at:]
        flat = coarse_in.astype(F32).reshape(window * group, wide).astype(BF16)
        local = jnp.dot(ac[...], flat, preferred_element_type=F32).reshape(rows, group, wide)
        out[comb_at:low_at, :] = jnp.sum(local * coarse_by.astype(F32), axis=1).astype(BF16)

    def strip(ref, chunk, r0, r1):
        parts = [ref[chunk * WIDE + i, r0:r1, :] for i in range(WIDE)]
        return jnp.concatenate(parts, axis=1)

    def summed(value, chunk, piece, part):
        lanes = slice(piece * LANE, (piece + 1) * LANE)
        at = (chunk * WIDE + piece) * LANE
        terms, kept = [], []
        for i in range(part * 8, part * 8 + 8):
            member = pert[i, :, at : at + LANE].astype(F32)
            product = member * value[level_at(i) : level_at(i) + members, lanes]
            total = product[0:8]
            for r in range(8, members, 8):
                total = total + product[r : r + 8]
            terms.append(total)
            kept.append(member)
        return fold(terms) + value[comb_at + part * 8 : comb_at + part * 8 + 8, lanes], kept

    when(-1, lambda: settle(filler(near), recv1.at[0]))
    when(1, lambda: settle(filler(near), recv1.at[1]))
    begin(late)
    localize(mc[...], cc[...], cp[own], fld)
    loads[6].wait()
    for chunk in range(fine // (WIDE * LANE)):
        interp = jnp.dot(fld[...], strip(matrix, chunk, 0, cells), preferred_element_type=F32)
        for piece in range(WIDE):
            for part in range(rows // 8):
                total, _ = summed(interp, chunk, piece, part)
                line[chunk * WIDE + piece, part * 8 : part * 8 + 8, :] = total
    def unpack(from_next, from_prev):
        low = lower(from_next.shape)
        nxt, prv = from_next.astype(F32), from_prev.astype(F32)
        return jnp.where(low, nxt, prv), turned(jnp.where(low, prv, nxt))

    def keep(level, value):
        value = value.astype(BF16)
        rim_m[level] = value[0:members]
        rim_c[level] = value[members : members + group]
        if HB <= level < HB + rows:
            rim_p[level - HB] = value[members + group :]

    settle(rt, recv1.at[4])
    for k, (a, b) in enumerate(pairs):
        va, vb = unpack(rt[0, k], rt[1, k])
        keep(HB + a, va)
        keep(HB + b, vb)
    when(-1, lambda: settle(rd.at[0], recv1.at[2]))
    when(1, lambda: settle(rd.at[1], recv1.at[3]))
    for floor in range(2):
        for k in range(half):
            va, vb = unpack(rd[floor, 0, k], rd[floor, 1, k])
            base = floor * (HB + rows)
            keep(base + k, va)
            keep(base + k + half, vb)
    localize(rim_m[...], rim_c[...], rim_p[...], fld_rim)
    for chunk in range(fine // (WIDE * LANE)):
        rim = strip(matrix, chunk, cells, span)
        interp = jnp.dot(fld_rim[...], rim, preferred_element_type=F32)
        for piece in range(WIDE):
            n = chunk * WIDE + piece
            totals = []
            for part in range(rows // 8):
                total, kept = summed(interp, chunk, piece, part)
                total = total + line[n, part * 8 : part * 8 + 8, :]
                totals.append(total)
                for r, member in enumerate(kept):
                    at = level_at(part * 8 + r)
                    adj[n, at : at + members, :] = (member * total[r : r + 1]).astype(BF16)
            adj[n, comb_at:low_at, :] = jnp.concatenate(totals, axis=0).astype(BF16)
        term = lax.dot_general(
            strip(adj, chunk, 0, rows * (members + 1)), rim, (((1,), (1,)), ((), ())),
            preferred_element_type=F32,
        )
        if chunk == 0:
            acc_rim[...] = term
        else:
            acc_rim[...] += term
    def packed_at(k):
        a = pairs[k][0]
        return (k - half) * members if a >= HB else pcomb_at + rows + k * members

    low = lower((members, LANE))
    for k, (a, b) in enumerate(pairs):
        value_a = acc_rim[level_at(a) : level_at(a) + members, :]
        value_b = turned(acc_rim[level_at(b) : level_at(b) + members, :])
        at = slice(packed_at(k), packed_at(k) + members)
        out_rim[1, at, :] = jnp.where(low, value_a, value_b).astype(BF16)
        out_rim[0, at, :] = jnp.where(low, value_b, value_a).astype(BF16)
    for side in range(2):
        out_rim[side, pcomb_at : pcomb_at + rows, :] = acc_rim[comb_at:low_at, :].astype(BF16)

    drain(pk, near + extra + 2 * half * kinds * LANE)
    begin(diag2 + tile2)
    for chunk in range(fine // (DEEP * LANE)):
        taken, met = [], []
        for i in range(DEEP):
            taken.append(adj[chunk * DEEP + i])
            met.append(matrix[chunk * DEEP + i, 0:cells, :])
        term = lax.dot_general(
            jnp.concatenate(taken, axis=1), jnp.concatenate(met, axis=1),
            (((1,), (1,)), ((), ())), preferred_element_type=F32,
        )
        if chunk == 0:
            acc_own[...] = term
        else:
            acc_own[...] += term
    out_own[...] = acc_own[...].astype(BF16)
    begin(lev2)
    when(-1, lambda: settle(filler(extra), recv1.at[5]))
    when(1, lambda: settle(filler(extra), recv1.at[6]))
    settle(r_tile, recv2.at[4])
    for floor, dl in ((0, -1), (1, 1)):
        when(dl, lambda floor=floor: settle(r_diag.at[floor], recv2.at[2 + floor]))
        when(dl, lambda floor=floor: settle(r_lev.at[floor], recv2.at[floor]))
    def zero_but(value, keep_low):
        low = lower(value.shape)
        return jnp.where(low, value, 0.0) if keep_low else jnp.where(low, 0.0, value)

    def joined(base, messages, at, swap):
        from_prev, from_next = messages[1, at, :].astype(F32), messages[0, at, :].astype(F32)
        if swap:
            from_prev, from_next = turned(from_prev), turned(from_next)
        parts = [base[:, i * LANE : (i + 1) * LANE] for i in range(cells // LANE)]
        parts[0] = parts[0] + zero_but(from_prev, True)
        parts[-1] = parts[-1] + zero_but(from_next, False)
        return parts

    def put(ref, r0, rn, parts):
        for i, part in enumerate(parts):
            ref[r0 : r0 + rn, i * LANE : (i + 1) * LANE] = part.astype(BF16)

    def stored_at(i):
        return HB * members + ((i - HB) * members if i >= HB else comb_at + i * members)

    for k, pair in enumerate(pairs):
        at = slice(packed_at(k), packed_at(k) + members)
        for swap, i in enumerate(pair):
            base = acc_own[level_at(i) : level_at(i) + members, :]
            put(xm, stored_at(i), members, joined(base, r_tile, at, swap))
    for floor in range(2):
        p0, o0 = (0, 0) if floor == 0 else (rows, rows)
        x0 = 0 if floor == 0 else HB * members + comb_at + HB * members
        for k in range(half):
            at = slice(p0 + k * members, p0 + (k + 1) * members)
            for swap in range(2):
                i = k + swap * half
                base = r_lev[floor, o0 + i * members : o0 + (i + 1) * members, :].astype(F32)
                put(xm, x0 + i * members, members, joined(base, r_diag.at[floor], at, swap))
    lines = []
    for floor, base in ((0, r_lev), (2, acc_own), (1, r_lev)):
        if floor == 2:
            parts = joined(acc_own[comb_at:low_at, :], r_tile, slice(pcomb_at, pcomb_at + rows), 0)
            chosen = range(rows)
        else:
            o0 = HB * members if floor == 0 else 0
            p0 = HB * members // 2 if floor == 0 else 0
            base = r_lev[floor, o0 : o0 + rows, :].astype(F32)
            parts = joined(base, r_diag.at[floor], slice(p0, p0 + rows), 0)
            chosen = range(rows - HB, rows) if floor == 0 else range(HB)
        lines += [[part[i : i + 1] for part in parts] for i in chosen]
    for level in range(0, window, 2):
        for i in range(cells // LANE):
            lanes = slice(i * LANE, (i + 1) * LANE)
            both = [cp[level + s, :, lanes].astype(F32) * lines[level + s][i] for s in range(2)]
            xc[level * group : (level + 2) * group, lanes] = jnp.concatenate(both, 0).astype(BF16)

    drain(out_rim, edge * cells + 2 * pedge * LANE)


def finish(xm, xc, bm, bc, mo_hbm, co_hbm, mo, co, sem):
    rows, members, cells = mo.shape
    group = co.shape[1]
    step = rows // 2
    copies = []
    for part in range(2):
        levels = pl.ds(part * step, step)
        at = slice(part * step * members, (part + 1) * step * members)
        value = jnp.dot(bm[at, :], xm[...], preferred_element_type=F32)
        mo[levels] = value.reshape(step, members, cells)
        copies.append(pltpu.make_async_copy(mo.at[levels], mo_hbm.at[levels], sem.at[part]))
        copies[-1].start()
    value = jnp.dot(bc[...], xc[...], preferred_element_type=F32)
    co[...] = value.reshape(rows, group, cells)
    copies.append(pltpu.make_async_copy(co, co_hbm, sem.at[2]))
    copies[-1].start()
    for copy in copies:
        copy.wait()


def solution(mesh):
    tiles, levs = mesh.shape["tile"], mesh.shape["lev"]

    def step(members_pert, coarse_pert, member_ctrl, coarse_ctrl, vert_loc, stencil, interp_w):
        rows, members, cells = member_ctrl.shape
        group = coarse_ctrl.shape[1]
        fine = members_pert.shape[2]
        levels, span, lines = rows + 2 * HB, cells + LANE, rows * (members + 1)
        edge = HB * members + rows
        comb_at, packed = dims(rows, members, group, cells)
        pedge = HB * members // 2 + rows
        hbm = pl.BlockSpec(memory_space=pl.ANY)
        kinds = members + 2 * group
        vmem = pl.BlockSpec(memory_space=pltpu.VMEM)
        results = pl.pallas_call(
            functools.partial(kernel, tiles, levs),
            out_shape=(
                pltpu.VMEM((levels * members, cells), BF16),
                pltpu.VMEM((levels * group, cells), BF16),
                pltpu.VMEM((rows * members, levels * members), BF16),
                pltpu.VMEM((rows * group, levels * group), BF16),
            ),
            in_specs=[hbm] * 7,
            out_specs=(vmem,) * 4,
            scratch_shapes=[
                pltpu.VMEM((levels, members, cells), BF16),
                pltpu.VMEM((levels, group, cells), BF16),
                pltpu.VMEM((levels, group, cells), BF16),
                pltpu.VMEM((rows, members, fine), BF16),
                pltpu.VMEM(vert_loc.shape, F32),
                pltpu.VMEM(stencil.shape, jnp.int32),
                pltpu.VMEM(interp_w.shape, BF16),
                pltpu.VMEM((fine // LANE, span, LANE), BF16),
                pltpu.VMEM((rows * members, levels * members), BF16),
                pltpu.VMEM((rows * group, levels * group), BF16),
                pltpu.VMEM((levels, members, LANE), BF16),
                pltpu.VMEM((levels, group, LANE), BF16),
                pltpu.VMEM((rows, group, LANE), BF16),
                pltpu.VMEM((2, rows // 2, kinds, LANE), BF16),
                pltpu.VMEM((2, rows // 2, kinds, LANE), BF16),
                pltpu.VMEM((2, 2, HB // 2, kinds, LANE), BF16),
                pltpu.VMEM((lines, cells), BF16),
                pltpu.VMEM((lines, LANE), BF16),
                pltpu.VMEM((fine // LANE, lines, LANE), BF16),
                pltpu.VMEM((fine // LANE, rows, LANE), F32),
                pltpu.VMEM((lines, LANE), F32),
                pltpu.VMEM((lines, cells), BF16),
                pltpu.VMEM((2, packed, LANE), BF16),
                pltpu.VMEM((lines, cells), F32),
                pltpu.VMEM((2, packed, LANE), BF16),
                pltpu.VMEM((2, edge, cells), BF16),
                pltpu.VMEM((2, 2, pedge, LANE), BF16),
                pltpu.SemaphoreType.DMA((7,)),
                pltpu.SemaphoreType.DMA((3,)),
                pltpu.SemaphoreType.DMA((7,)),
                pltpu.SemaphoreType.DMA((5,)),
            ],
            compiler_params=pltpu.CompilerParams(
                collective_id=0, has_side_effects=True, vmem_limit_bytes=56 * 1024 * 1024
            ),
        )(members_pert, coarse_pert, member_ctrl, coarse_ctrl, vert_loc, stencil, interp_w)
        return pl.pallas_call(
            finish,
            out_shape=(
                jax.ShapeDtypeStruct((rows, members, cells), F32),
                jax.ShapeDtypeStruct((rows, group, cells), F32),
            ),
            in_specs=[vmem] * 4,
            out_specs=(hbm, hbm),
            scratch_shapes=[
                pltpu.VMEM((rows, members, cells), F32),
                pltpu.VMEM((rows, group, cells), F32),
                pltpu.SemaphoreType.DMA((3,)),
            ],
            compiler_params=pltpu.CompilerParams(vmem_limit_bytes=4 * 1024 * 1024),
        )(*results)

    in_specs = (
        P("lev", None, "tile"),
        P("lev", None, "tile"),
        P("lev", None, "tile"),
        P("lev", None, "tile"),
        P(),
        P(None, "tile"),
        P(None, "tile"),
    )
    out_specs = (P("lev", None, "tile"), P("lev", None, "tile"))
    return jax.shard_map(step, mesh=mesh, in_specs=in_specs, out_specs=out_specs, check_vma=False)
```

time: 20.5 us -> 18.8 us (0.917)
  Pallas kernels: 19.7 us -> 18 us
    pallas_call x1, Pallas kernels: 18.9 us -> 17.1 us  [step(): pl.pallas_call(functools.partial(kernel, tiles, levs), out_shape=(pltpu.V...]
    pallas_call x1, Pallas kernels: 0.76 us -> 0.97 us  [step(): pl.pallas_call(finish, out_shape=(jax.ShapeDtypeStruct((rows, members, ce...]
where the time goes in v1:
time: 18.8 us; the launch traced here: 18.7 us
  Pallas kernels  18 us (96%)
  between operations  0.64 us (3%)
    pallas_call x1, Pallas kernels, step(): pl.pallas_call(functools.partial(kernel, tiles, levs), out_shape=(pltpu.V...  17.1 us
    pallas_call x1, Pallas kernels, step(): pl.pallas_call(finish, out_shape=(jax.ShapeDtypeStruct((rows, members, ce...  0.97 us

profile of v1, /device:TPU:0, one launch (start us, length us, event | category | flops | bytes accessed | tf_op | source)
XLA Modules:
  0.0 18.7 jit_solution(7732935708983424163)
XLA Ops:
  0.6 17.1 %shard_map.86 = (bf16[384,256]{1,0:T(8,128)(2,1)S(1)}, bf16[192,256]{1,0:T(8,128)(2,1)S(1)}, bf16[256,384]{1,0:T(8,128)(2,1)S(1)}, bf16[128,192]{1,0:T(8,128)(2,1)S(1)}) custom-call(bf16[16,16,4096]{2,1,0:T(8,128)(2,1)} %pert_hbm.1, bf16[16,8,256]{2,1,0:T(8,128)(2,1)} %cp_hbm.1, bf16[16,16,256]{2,1,0:T(8,128)(2,1)} %mc_hbm.1, bf16[16,8,256]{2,1,0:T(8,128)(2,1)} %cc_hbm.1, ...), custom_call_target="tpu_custom_call" | custom-call | tf_op jit(solution)/shard_map/pallas_call | solution.py:472
  17.7 1.0 %shard_map.87 = (f32[16,16,256]{2,1,0:T(8,128)}, f32[16,8,256]{2,1,0:T(8,128)}) custom-call(bf16[384,256]{1,0:T(8,128)(2,1)S(1)} %get-tuple-element.6.xm, bf16[192,256]{1,0:T(8,128)(2,1)S(1)} %get-tuple-element.7.xc, bf16[256,384]{1,0:T(8,128)(2,1)S(1)} %get-tuple-element.8.bm, bf16[128,192]{1,0:T(8,128)(2,1)S(1)} %get-tuple-element.9.bc), custom_call_target="tpu_custom_call" | custom-call | tf_op jit(solution)/shard_map/pallas_call | solution.py:519

commit v2 on v1

--- a/solution.py
+++ b/solution.py
@@ -10,8 +10,7 @@
 HB = 4
 CW = 64
 LANE = 128
-WIDE = 8
-DEEP = 8
+WIDE = 2
 MESH = pl.DeviceIdType.MESH
 F32 = jnp.float32
 BF16 = jnp.bfloat16
@@ -24,10 +23,8 @@
     return [(b + k, b + k + half) for b in range(0, rows, HB) for k in range(half)]
 
 
-def dims(rows, members, group, cells):
-    comb_at = (rows - HB) * members
-    packed = comb_at // 2 + rows + HB * members // 2
-    return comb_at, packed
+def order_of(rows):
+    return list(range(rows - HB, rows)) + list(range(HB)) + list(range(HB, rows - HB))
 
 
 def fold(values):
@@ -41,11 +38,22 @@
     return values[0]
 
 
-def kernel(
-    tiles, levs, pert_hbm, cp_hbm, mc_hbm, cc_hbm, vert_hbm, st_hbm, w_hbm, xm, xc, bm, bc,
+def kernel(tiles, levs, *refs):
+    rows, members, cells = refs[2].shape
+    group = refs[3].shape[1]
+    whole, coarse, few = rows * (members + 1), rows * group, rows
+    scopes = [
+        pltpu.ACC(mxu)((height, cells), F32)
+        for height in (whole, whole, whole, coarse, few) for mxu in range(2)
+    ]
+    pl.run_scoped(lambda *sums: body(tiles, levs, sums, *refs), *scopes)
+
+
+def body(
+    tiles, levs, sums, pert_hbm, cp_hbm, mc_hbm, cc_hbm, vert_hbm, st_hbm, w_hbm, xm, xc, bm, bc,
     mc, cc, cp, pert, vert, st, w, matrix, am, ac, rim_m, rim_c, rim_p, pk, rt, rd,
     fld, fld_rim, adj, line, acc_rim, out_own, out_rim, acc_own, r_tile, r_lev, r_diag,
-    load_sem, send, recv1, recv2,
+    load_sem, send, recv1, recv2, ready,
 ):
     rows, members, cells = mc_hbm.shape
     group = cc_hbm.shape[1]
@@ -55,18 +63,28 @@
     window = rows + 2 * HB
     edge = HB * members + rows
     last = cells - LANE
-    comb_at, packed = dims(rows, members, group, cells)
+    comb_at, low_at = HB * members, HB * members + rows
+    whole = rows * (members + 1)
     pcomb_at = comb_at // 2
-    low_at = comb_at + rows
-    tail_at = comb_at - HB * members
-    ptail_at = pcomb_at - HB * members // 2
-    pedge = HB * members // 2 + rows
+    pedge = pcomb_at + rows
+    order = order_of(rows)
     pairs = pairs_of(rows)
     half = HB // 2
     kinds = members + 2 * group
 
     def level_at(i):
-        return (i - HB) * members if i >= HB else low_at + i * members
+        place = order.index(i)
+        return place * members + (rows if place >= HB else 0)
+
+    assert cells == WIDE * LANE and window * members <= 2 * cells and window * group <= cells
+    ahead, behind, rim_sum, coarse_sum, few_sum = (sums[i : i + 2] for i in range(0, 10, 2))
+    turns = [0, 0]
+
+    def product(into, mxu, left, right, transpose=False):
+        turn = turns[mxu]
+        turns[mxu] = 1 - turn
+        pltpu.matmul_push_rhs(right, staging_register=turn, mxu_index=mxu, transpose=transpose)
+        pltpu.matmul_acc_lhs(into[mxu], left, load_staged_rhs=turn)
 
     t = lax.axis_index("tile")
     v = lax.axis_index("lev")
@@ -83,6 +101,10 @@
     def begin(copies):
         for dl, copy in copies:
             when(dl, copy.start)
+
+    def start_first(copies):
+        for dl, copy in copies:
+            pl.when(jnp.logical_and(v == 0, levs > 1))(copy.start)
 
     def settle(ref, sem):
         pltpu.make_async_copy(ref, ref, sem).wait()
@@ -108,16 +130,25 @@
     for load in loads[:3]:
         load.start()
 
+    below = {-1: t > 0, 1: t == tiles - 1}
+
+    def signal(sem, dt, dl):
+        pl.semaphore_signal(sem, inc=1, device_id=(beside[dt], v + dl), device_id_type=MESH)
+
     barrier = pltpu.get_barrier_semaphore()
-    for dt, dl in DIRECTIONS:
-        when(
-            dl,
-            lambda dt=dt, dl=dl: pl.semaphore_signal(
-                barrier, inc=1, device_id=(beside[dt], v + dl), device_id_type=MESH
-            ),
-        )
+    for dt in (-1, 1):
+        pl.when(jnp.logical_not(below[dt]))(lambda dt=dt: signal(barrier, dt, 0))
+    for dt in (-1, 0, 1):
+        when(1, lambda dt=dt: signal(barrier, dt, 1))
+        pl.when(v == 1)(lambda dt=dt: signal(barrier, dt, -1))
     for load in loads[3:]:
         load.start()
+    lower_tiles = jnp.where(t > 0, 1, 0) + jnp.where(t == tiles - 1, 1, 0)
+    pl.semaphore_wait(barrier, lower_tiles + (3 if levs > 1 else 0))
+    for dt in (-1, 1):
+        pl.when(below[dt])(lambda dt=dt: signal(ready.at[0], dt, 0))
+    for dt in (-1, 0, 1):
+        pl.when(v > 1)(lambda dt=dt: signal(ready.at[1], dt, -1))
 
     def remote(src, dst, send_at, recv_at, dt, dl):
         return dl, pltpu.make_async_remote_copy(
@@ -128,8 +159,8 @@
     level_src = {1: rows, -1: HB}
     level_dst = {1: 0, -1: HB + rows}
     entry_src = {1: len(pairs) - half, -1: 0}
-    tile_row = {1: ptail_at, -1: pcomb_at}
-    lev_row = {1: tail_at, -1: comb_at}
+    tile_row = {1: 0, -1: pcomb_at}
+    lev_row = {1: 0, -1: comb_at}
     lev1, late, tile1, diag1, tile2, diag2, lev2 = [], [], [], [], [], [], []
     for dl in (-1, 1):
         floor = (1 - dl) // 2
@@ -143,7 +174,8 @@
         for dt in (-1, 1):
             side = (1 + dt) // 2
             diag1.append(remote(
-                pk.at[side, pl.ds(entry_src[dl], half)], rd.at[floor, side],
+                pk.at[side, pl.ds(entry_src[dl], half), pl.ds(0, members + group)],
+                rd.at[floor, side],
                 send.at[1 + floor], recv1.at[2 + floor], dt, dl))
             diag2.append(remote(
                 out_rim.at[side, pl.ds(tile_row[dl], pedge)], r_diag.at[floor, side],
@@ -179,9 +211,8 @@
 
     for load in loads[:3]:
         load.wait()
-    neighbours = 2 + 3 * jnp.where(v > 0, 1, 0) + 3 * jnp.where(v < levs - 1, 1, 0)
-    pl.semaphore_wait(barrier, neighbours)
-    begin(lev1)
+    begin([x for x in lev1 if x[0] < 0])
+    start_first([x for x in lev1 if x[0] > 0])
     for k, (a, b) in enumerate(pairs):
         for buf, r0, rn in ((mc, 0, members), (cc, members, group), (cp, members + group, group)):
             low = lower((rn, LANE))
@@ -189,7 +220,10 @@
             far_a, far_b = (buf[HB + i, :, last:].astype(F32) for i in (a, b))
             pk[0, k, r0 : r0 + rn, :] = jnp.where(low, near_a, turned(near_b)).astype(BF16)
             pk[1, k, r0 : r0 + rn, :] = jnp.where(low, turned(far_b), far_a).astype(BF16)
-    begin(diag1 + tile1)
+    begin([x for x in diag1 if x[0] < 0])
+    start_first([x for x in diag1 if x[0] > 0])
+    for dt, (dl, copy) in zip((-1, 1), tile1):
+        pl.when(below[dt])(copy.start)
     for load in loads[3:6]:
         load.wait()
     pack = 16
@@ -212,88 +246,158 @@
             matrix[step, block * pack : (block + 1) * pack, :] = value
         return carry
 
-    lax.fori_loop(0, fine // LANE, build, 0)
+    steps = fine // LANE
+    lax.fori_loop(0, steps // 2, build, 0)
+    pl.when(t < tiles - 1)(lambda: pl.semaphore_wait(ready.at[0], 2 - lower_tiles))
+    for dt, (dl, copy) in zip((-1, 1), tile1):
+        pl.when(jnp.logical_not(below[dt]))(copy.start)
+    lax.fori_loop(steps // 2, steps, build, 0)
+    inner = jnp.logical_and(v > 0, v < levs - 1)
+    pl.when(inner)(lambda: pl.semaphore_wait(ready.at[1], 3))
+    for dl, copy in lev1 + diag1:
+        if dl > 0:
+            pl.when(inner)(copy.start)
 
     factors = vert[...].astype(BF16)
-    level_k = lax.broadcasted_iota(jnp.int32, (rows, total_levels), 1)
-    level_i = lax.broadcasted_iota(jnp.int32, (rows, total_levels), 0)
+    factors = jnp.concatenate(
+        [factors, jnp.zeros((total_levels, cells - total_levels), BF16)], axis=1)
+    factors = jnp.concatenate(
+        [factors, jnp.zeros((cells - total_levels, cells), BF16)], axis=0)
+    level_k = lax.broadcasted_iota(jnp.int32, (rows, cells), 1)
+    level_i = lax.broadcasted_iota(jnp.int32, (rows, cells), 0)
     pick = jnp.where(level_k == first + level_i, 1.0, 0.0).astype(BF16)
-    forward = jnp.dot(pick, factors, preferred_element_type=F32).astype(BF16)
-    backward = lax.dot_general(
-        pick, factors, (((1,), (1,)), ((), ())), preferred_element_type=F32
-    ).astype(BF16)
-
-    def spread_out(source, height, offset):
-        wide = window * height
-        lane = lax.broadcasted_iota(jnp.int32, (total_levels, wide), 1) // height
-        row = lax.broadcasted_iota(jnp.int32, (total_levels, wide), 0)
-        chosen = jnp.where(row == first + offset(lane), 1.0, 0.0).astype(BF16)
-        lines = jnp.dot(source, chosen, preferred_element_type=F32)
-        at = lax.broadcasted_iota(jnp.int32, (height, wide), 1) % height
-        mask = at == lax.broadcasted_iota(jnp.int32, (height, wide), 0)
-        return [jnp.where(mask, lines[i : i + 1], 0.0) for i in range(rows)]
+    product(few_sum, 0, pick, factors)
+    product(few_sum, 1, pick, factors, transpose=True)
+    forward = pltpu.matmul_pop(few_sum[0]).astype(BF16)
+    backward = pltpu.matmul_pop(few_sum[1]).astype(BF16)
+
+    def spread_out(source, height, offset, mxu, base):
+        shape = (total_levels, cells)
+        seg = (lax.broadcasted_iota(jnp.int32, shape, 1) + base) // height
+        row = lax.broadcasted_iota(jnp.int32, shape, 0)
+        hit = jnp.logical_and(row == first + offset(seg), seg < window)
+        chosen = jnp.where(hit, 1.0, 0.0).astype(BF16)
+        chosen = jnp.concatenate([chosen, jnp.zeros((cells - total_levels, cells), BF16)], axis=0)
+        product(few_sum, mxu, source, chosen)
+        return pltpu.matmul_pop(few_sum[mxu])
+
+    def blocks_of(lines, height):
+        at = lax.broadcasted_iota(jnp.int32, (height, LANE), 1) % height
+        mask = at == lax.broadcasted_iota(jnp.int32, (height, LANE), 0)
+        return [
+            [
+                jnp.where(mask, line[i : i + 1, p : p + LANE], 0.0)
+                for line in lines for p in range(0, cells, LANE)
+            ]
+            for i in range(rows)
+        ]
 
     def natural(seg):
         return seg - HB
 
     def stored(seg):
-        return jnp.where(
-            seg < HB, seg - HB,
-            jnp.where(seg < rows, seg, jnp.where(seg < rows + HB, seg - rows, seg - HB)),
-        )
-
-    order = list(range(HB, rows)) + list(range(HB))
-    blocks = spread_out(forward, members, natural)
-    for place, i in enumerate(order):
-        am[place * members : (place + 1) * members, :] = blocks[i].astype(BF16)
-    blocks = spread_out(backward, members, stored)
-    for i in range(rows):
-        bm[i * members : (i + 1) * members, :] = blocks[i].astype(BF16)
-    for out, source in ((ac, forward), (bc, backward)):
-        blocks = spread_out(source, group, natural)
+        inner = jnp.where(seg < 2 * HB, seg + rows - 2 * HB, seg - 2 * HB)
+        return jnp.where(jnp.logical_or(seg < HB, seg >= rows + HB), seg - HB, inner)
+
+    lines = [spread_out(forward, members, natural, m, m * cells) for m in range(2)]
+    for i, pieces in enumerate(blocks_of(lines, members)):
+        for p, piece in enumerate(pieces):
+            am[p, level_at(i) : level_at(i) + members, :] = piece.astype(BF16)
+    for p in range(am.shape[0]):
+        am[p, comb_at:low_at, :] = jnp.zeros((rows, LANE), BF16)
+    lines = [spread_out(backward, members, stored, m, m * cells) for m in range(2)]
+    for i, pieces in enumerate(blocks_of(lines, members)):
+        for p, piece in enumerate(pieces):
+            if p * LANE < bm.shape[1]:
+                bm[i * members : (i + 1) * members, p * LANE : (p + 1) * LANE] = piece.astype(BF16)
+    coarse_lines = [
+        [spread_out(source, group, natural, m, 0)] for m, source in enumerate((forward, backward))
+    ]
+    for out, lines in zip((ac, bc), coarse_lines):
+        blocks = blocks_of(lines, group)
+        if out is ac:
+            blocks = [blocks[i] for i in order]
         for i in range(0, rows, 2):
-            both = jnp.concatenate(blocks[i : i + 2], axis=0)
-            out[i * group : (i + 2) * group, :] = both.astype(BF16)
+            for p in range(cells // LANE):
+                both = jnp.concatenate([blocks[i][p], blocks[i + 1][p]], axis=0)
+                out[p, i * group : (i + 2) * group, :] = both.astype(BF16)
+
+    def side_by_side(ref, p0=0):
+        return jnp.concatenate([ref[p0], ref[p0 + 1]], axis=1)
+
+    def square(value):
+        height, wide = value.shape
+        if wide < cells:
+            value = jnp.concatenate([value, jnp.zeros((height, cells - wide), BF16)], axis=1)
+        if height < cells:
+            value = jnp.concatenate([value, jnp.zeros((cells - height, cells), BF16)], axis=0)
+        return value
 
     def localize(members_in, coarse_in, coarse_by, out):
         wide = members_in.shape[-1]
-        value = jnp.dot(
-            am[...], members_in.reshape(window * members, wide), preferred_element_type=F32
-        ).astype(BF16)
-        out[0:comb_at, :] = value[0:comb_at]
-        out[low_at:, :] = value[comb_at:]
+        flat = members_in.reshape(window * members, wide)
+        product(ahead, 0, side_by_side(am), square(flat[0:cells]))
+        product(ahead, 1, side_by_side(am, 2), square(flat[cells:]))
         flat = coarse_in.astype(F32).reshape(window * group, wide).astype(BF16)
-        local = jnp.dot(ac[...], flat, preferred_element_type=F32).reshape(rows, group, wide)
-        out[comb_at:low_at, :] = jnp.sum(local * coarse_by.astype(F32), axis=1).astype(BF16)
+        product(coarse_sum, 1, side_by_side(ac), square(flat))
+        value = pltpu.matmul_pop(ahead[0]) + pltpu.matmul_pop(ahead[1])
+        local = pltpu.matmul_pop(coarse_sum[1])
+        for p in range(wide // LANE):
+            lanes = slice(p * LANE, (p + 1) * LANE)
+            part = value[:, lanes].astype(BF16)
+            out[p, 0:comb_at, :] = part[0:comb_at]
+            out[p, low_at:, :] = part[low_at:]
+            mixed = [
+                local[place * group : (place + 1) * group, lanes] * coarse_by[i, :, lanes].astype(F32)
+                for place, i in enumerate(order)
+            ]
+            sums = [fold(mixed[g : g + 8]) for g in range(0, rows, 8)]
+            out[p, comb_at:low_at, :] = jnp.concatenate(sums, axis=0).astype(BF16)
 
     def strip(ref, chunk, r0, r1):
         parts = [ref[chunk * WIDE + i, r0:r1, :] for i in range(WIDE)]
         return jnp.concatenate(parts, axis=1)
 
-    def summed(value, chunk, piece, part):
-        lanes = slice(piece * LANE, (piece + 1) * LANE)
-        at = (chunk * WIDE + piece) * LANE
-        terms, kept = [], []
-        for i in range(part * 8, part * 8 + 8):
-            member = pert[i, :, at : at + LANE].astype(F32)
-            product = member * value[level_at(i) : level_at(i) + members, lanes]
-            total = product[0:8]
-            for r in range(8, members, 8):
-                total = total + product[r : r + 8]
-            terms.append(total)
-            kept.append(member)
-        return fold(terms) + value[comb_at + part * 8 : comb_at + part * 8 + 8, lanes], kept
+    def summed(value, chunk, part):
+        terms = [[] for _ in range(WIDE)]
+        for i in order[part * 8 : part * 8 + 8]:
+            for piece in range(WIDE):
+                lanes = slice(piece * LANE, (piece + 1) * LANE)
+                at = (chunk * WIDE + piece) * LANE
+                member = pert[i, :, at : at + LANE].astype(F32)
+                product_ = member * value[level_at(i) : level_at(i) + members, lanes]
+                total = product_[0:8]
+                for r in range(8, members, 8):
+                    total = total + product_[r : r + 8]
+                terms[piece].append(total)
+        at = comb_at + part * 8
+        return [
+            fold(terms[piece]) + value[at : at + 8, piece * LANE : (piece + 1) * LANE]
+            for piece in range(WIDE)
+        ]
 
     when(-1, lambda: settle(filler(near), recv1.at[0]))
     when(1, lambda: settle(filler(near), recv1.at[1]))
     begin(late)
     localize(mc[...], cc[...], cp[own], fld)
     loads[6].wait()
-    for chunk in range(fine // (WIDE * LANE)):
-        interp = jnp.dot(fld[...], strip(matrix, chunk, 0, cells), preferred_element_type=F32)
-        for piece in range(WIDE):
-            for part in range(rows // 8):
-                total, _ = summed(interp, chunk, piece, part)
+    chunks = fine // (WIDE * LANE)
+
+    def slot(chunk):
+        return (ahead, behind)[(chunk // 2) % 2], chunk % 2
+
+    def first_product(chunk):
+        product(*slot(chunk), side_by_side(fld), strip(matrix, chunk, 0, cells))
+
+    for chunk in range(min(4, chunks)):
+        first_product(chunk)
+    for chunk in range(chunks):
+        into, mxu = slot(chunk)
+        interp = pltpu.matmul_pop(into[mxu])
+        if chunk + 4 < chunks:
+            first_product(chunk + 4)
+        for part in range(rows // 8):
+            for piece, total in enumerate(summed(interp, chunk, part)):
                 line[chunk * WIDE + piece, part * 8 : part * 8 + 8, :] = total
     def unpack(from_next, from_prev):
         low = lower(from_next.shape)
@@ -321,31 +425,50 @@
             keep(base + k, va)
             keep(base + k + half, vb)
     localize(rim_m[...], rim_c[...], rim_p[...], fld_rim)
-    for chunk in range(fine // (WIDE * LANE)):
-        rim = strip(matrix, chunk, cells, span)
-        interp = jnp.dot(fld_rim[...], rim, preferred_element_type=F32)
+    rim_fields = jnp.concatenate([fld_rim[0], jnp.zeros((whole, cells - LANE), BF16)], axis=1)
+    def rim_of(chunk):
+        return square(strip(matrix, chunk, cells, span))
+
+    def rim_product(chunk):
+        product(*slot(chunk), rim_fields, rim_of(chunk))
+
+    def own_product(chunk):
+        product(
+            ahead, chunk % 2, strip(adj, chunk, 0, whole), strip(matrix, chunk, 0, cells),
+            transpose=True,
+        )
+
+    for chunk in range(min(4, chunks)):
+        rim_product(chunk)
+    for chunk in range(chunks):
+        into, mxu = slot(chunk)
+        interp = pltpu.matmul_pop(into[mxu])
+        if chunk + 4 < chunks:
+            rim_product(chunk + 4)
+        totals = [[] for _ in range(WIDE)]
+        for part in range(rows // 8):
+            for piece, total in enumerate(summed(interp, chunk, part)):
+                n = chunk * WIDE + piece
+                total = total + line[n, part * 8 : part * 8 + 8, :]
+                totals[piece].append(total)
+                for r, i in enumerate(order[part * 8 : part * 8 + 8]):
+                    by = jnp.broadcast_to(total[r : r + 1], (members, LANE)).astype(BF16)
+                    at = level_at(i)
+                    lanes = slice(n * LANE, (n + 1) * LANE)
+                    adj[n, at : at + members, :] = pert[i, :, lanes] * by
         for piece in range(WIDE):
-            n = chunk * WIDE + piece
-            totals = []
-            for part in range(rows // 8):
-                total, kept = summed(interp, chunk, piece, part)
-                total = total + line[n, part * 8 : part * 8 + 8, :]
-                totals.append(total)
-                for r, member in enumerate(kept):
-                    at = level_at(part * 8 + r)
-                    adj[n, at : at + members, :] = (member * total[r : r + 1]).astype(BF16)
-            adj[n, comb_at:low_at, :] = jnp.concatenate(totals, axis=0).astype(BF16)
-        term = lax.dot_general(
-            strip(adj, chunk, 0, rows * (members + 1)), rim, (((1,), (1,)), ((), ())),
-            preferred_element_type=F32,
-        )
-        if chunk == 0:
-            acc_rim[...] = term
-        else:
-            acc_rim[...] += term
+            both = jnp.concatenate(totals[piece], axis=0)
+            adj[chunk * WIDE + piece, comb_at:low_at, :] = both.astype(BF16)
+        product(rim_sum, mxu, strip(adj, chunk, 0, whole), rim_of(chunk), transpose=True)
+    early = min(4, chunks)
+    for chunk in range(early):
+        own_product(chunk)
+    back = pltpu.matmul_pop(rim_sum[0]) + pltpu.matmul_pop(rim_sum[1])
+    acc_rim[...] = back[:, 0:LANE]
     def packed_at(k):
-        a = pairs[k][0]
-        return (k - half) * members if a >= HB else pcomb_at + rows + k * members
+        place = order.index(pairs[k][0])
+        entry = place // HB * half + place % HB
+        return entry * members + (rows if place >= HB else 0)
 
     low = lower((members, LANE))
     for k, (a, b) in enumerate(pairs):
@@ -357,21 +480,11 @@
     for side in range(2):
         out_rim[side, pcomb_at : pcomb_at + rows, :] = acc_rim[comb_at:low_at, :].astype(BF16)
 
-    drain(pk, near + extra + 2 * half * kinds * LANE)
+    drain(pk, near + extra + 2 * half * (members + group) * LANE)
     begin(diag2 + tile2)
-    for chunk in range(fine // (DEEP * LANE)):
-        taken, met = [], []
-        for i in range(DEEP):
-            taken.append(adj[chunk * DEEP + i])
-            met.append(matrix[chunk * DEEP + i, 0:cells, :])
-        term = lax.dot_general(
-            jnp.concatenate(taken, axis=1), jnp.concatenate(met, axis=1),
-            (((1,), (1,)), ((), ())), preferred_element_type=F32,
-        )
-        if chunk == 0:
-            acc_own[...] = term
-        else:
-            acc_own[...] += term
+    for chunk in range(early, chunks):
+        own_product(chunk)
+    acc_own[...] = pltpu.matmul_pop(ahead[0]) + pltpu.matmul_pop(ahead[1])
     out_own[...] = acc_own[...].astype(BF16)
     begin(lev2)
     when(-1, lambda: settle(filler(extra), recv1.at[5]))
@@ -379,6 +492,7 @@
     settle(r_tile, recv2.at[4])
     for floor, dl in ((0, -1), (1, 1)):
         when(dl, lambda floor=floor: settle(r_diag.at[floor], recv2.at[2 + floor]))
+    for floor, dl in ((0, -1), (1, 1)):
         when(dl, lambda floor=floor: settle(r_lev.at[floor], recv2.at[floor]))
     def zero_but(value, keep_low):
         low = lower(value.shape)
@@ -398,7 +512,7 @@
             ref[r0 : r0 + rn, i * LANE : (i + 1) * LANE] = part.astype(BF16)
 
     def stored_at(i):
-        return HB * members + ((i - HB) * members if i >= HB else comb_at + i * members)
+        return (HB + order.index(i)) * members
 
     for k, pair in enumerate(pairs):
         at = slice(packed_at(k), packed_at(k) + members)
@@ -407,7 +521,7 @@
             put(xm, stored_at(i), members, joined(base, r_tile, at, swap))
     for floor in range(2):
         p0, o0 = (0, 0) if floor == 0 else (rows, rows)
-        x0 = 0 if floor == 0 else HB * members + comb_at + HB * members
+        x0 = 0 if floor == 0 else (HB + rows) * members
         for k in range(half):
             at = slice(p0 + k * members, p0 + (k + 1) * members)
             for swap in range(2):
@@ -415,16 +529,16 @@
                 base = r_lev[floor, o0 + i * members : o0 + (i + 1) * members, :].astype(F32)
                 put(xm, x0 + i * members, members, joined(base, r_diag.at[floor], at, swap))
     lines = []
-    for floor, base in ((0, r_lev), (2, acc_own), (1, r_lev)):
+    for floor in (0, 2, 1):
         if floor == 2:
             parts = joined(acc_own[comb_at:low_at, :], r_tile, slice(pcomb_at, pcomb_at + rows), 0)
-            chosen = range(rows)
+            chosen = [order.index(i) for i in range(rows)]
         else:
-            o0 = HB * members if floor == 0 else 0
-            p0 = HB * members // 2 if floor == 0 else 0
+            o0 = comb_at if floor == 0 else 0
+            p0 = pcomb_at if floor == 0 else 0
             base = r_lev[floor, o0 : o0 + rows, :].astype(F32)
             parts = joined(base, r_diag.at[floor], slice(p0, p0 + rows), 0)
-            chosen = range(rows - HB, rows) if floor == 0 else range(HB)
+            chosen = range(HB) if floor == 0 else range(HB, 2 * HB)
         lines += [[part[i : i + 1] for part in parts] for i in chosen]
     for level in range(0, window, 2):
         for i in range(cells // LANE):
@@ -447,7 +561,8 @@
         mo[levels] = value.reshape(step, members, cells)
         copies.append(pltpu.make_async_copy(mo.at[levels], mo_hbm.at[levels], sem.at[part]))
         copies[-1].start()
-    value = jnp.dot(bc[...], xc[...], preferred_element_type=F32)
+    left = jnp.concatenate([bc[0], bc[1]], axis=1)[:, 0 : xc.shape[0]]
+    value = jnp.dot(left, xc[...], preferred_element_type=F32)
     co[...] = value.reshape(rows, group, cells)
     copies.append(pltpu.make_async_copy(co, co_hbm, sem.at[2]))
     copies[-1].start()
@@ -464,8 +579,8 @@
         fine = members_pert.shape[2]
         levels, span, lines = rows + 2 * HB, cells + LANE, rows * (members + 1)
         edge = HB * members + rows
-        comb_at, packed = dims(rows, members, group, cells)
         pedge = HB * members // 2 + rows
+        packed = rows * members // 2 + rows
         hbm = pl.BlockSpec(memory_space=pl.ANY)
         kinds = members + 2 * group
         vmem = pl.BlockSpec(memory_space=pltpu.VMEM)
@@ -475,7 +590,7 @@
                 pltpu.VMEM((levels * members, cells), BF16),
                 pltpu.VMEM((levels * group, cells), BF16),
                 pltpu.VMEM((rows * members, levels * members), BF16),
-                pltpu.VMEM((rows * group, levels * group), BF16),
+                pltpu.VMEM((cells // LANE, rows * group, LANE), BF16),
             ),
             in_specs=[hbm] * 7,
             out_specs=(vmem,) * 4,
@@ -488,16 +603,16 @@
                 pltpu.VMEM(stencil.shape, jnp.int32),
                 pltpu.VMEM(interp_w.shape, BF16),
                 pltpu.VMEM((fine // LANE, span, LANE), BF16),
-                pltpu.VMEM((rows * members, levels * members), BF16),
-                pltpu.VMEM((rows * group, levels * group), BF16),
+                pltpu.VMEM((2 * cells // LANE, lines, LANE), BF16),
+                pltpu.VMEM((cells // LANE, rows * group, LANE), BF16),
                 pltpu.VMEM((levels, members, LANE), BF16),
                 pltpu.VMEM((levels, group, LANE), BF16),
                 pltpu.VMEM((rows, group, LANE), BF16),
                 pltpu.VMEM((2, rows // 2, kinds, LANE), BF16),
                 pltpu.VMEM((2, rows // 2, kinds, LANE), BF16),
-                pltpu.VMEM((2, 2, HB // 2, kinds, LANE), BF16),
-                pltpu.VMEM((lines, cells), BF16),
-                pltpu.VMEM((lines, LANE), BF16),
+                pltpu.VMEM((2, 2, HB // 2, members + group, LANE), BF16),
+                pltpu.VMEM((cells // LANE, lines, LANE), BF16),
+                pltpu.VMEM((1, lines, LANE), BF16),
                 pltpu.VMEM((fine // LANE, lines, LANE), BF16),
                 pltpu.VMEM((fine // LANE, rows, LANE), F32),
                 pltpu.VMEM((lines, LANE), F32),
@@ -511,6 +626,7 @@
                 pltpu.SemaphoreType.DMA((3,)),
                 pltpu.SemaphoreType.DMA((7,)),
                 pltpu.SemaphoreType.DMA((5,)),
+                pltpu.SemaphoreType.REGULAR((2,)),
             ],
             compiler_params=pltpu.CompilerParams(
                 collective_id=0, has_side_effects=True, vmem_limit_bytes=56 * 1024 * 1024

time: 18.8 us -> 16.4 us (0.87)
  Pallas kernels: 18 us -> 15.6 us
    pallas_call x1, Pallas kernels: 17.1 us -> 14.7 us  [step(): pl.pallas_call(functools.partial(kernel, tiles, levs), out_shape=(pltpu.V...]
where the time goes in v2:
time: 16.4 us; the launch traced here: 16.3 us
  Pallas kernels  15.6 us (95%)
  between operations  0.64 us (4%)
    pallas_call x1, Pallas kernels, step(): pl.pallas_call(functools.partial(kernel, tiles, levs), out_shape=(pltpu.V...  14.7 us
    pallas_call x1, Pallas kernels, step(): pl.pallas_call(finish, out_shape=(jax.ShapeDtypeStruct((rows, members, ce...  0.97 us

profile of v2, /device:TPU:0, one launch (start us, length us, event | category | flops | bytes accessed | tf_op | source)
XLA Modules:
  0.0 16.3 jit_solution(7030266687662430201)
XLA Ops:
  0.6 14.7 %shard_map.86 = (bf16[384,256]{1,0:T(8,128)(2,1)S(1)}, bf16[192,256]{1,0:T(8,128)(2,1)S(1)}, bf16[256,384]{1,0:T(8,128)(2,1)S(1)}, bf16[2,128,128]{2,1,0:T(8,128)(2,1)S(1)}) custom-call(bf16[16,16,4096]{2,1,0:T(8,128)(2,1)} %refs_0_.1, bf16[16,8,256]{2,1,0:T(8,128)(2,1)} %refs_1_.1, bf16[16,16,256]{2,1,0:T(8,128)(2,1)} %refs_2_.1, ...), custom_call_target="tpu_custom_call" | custom-call | tf_op jit(solution)/shard_map/pallas_call | solution.py:587
  15.3 1.0 %shard_map.87 = (f32[16,16,256]{2,1,0:T(8,128)}, f32[16,8,256]{2,1,0:T(8,128)}) custom-call(bf16[384,256]{1,0:T(8,128)(2,1)S(1)} %get-tuple-element.6.xm, bf16[192,256]{1,0:T(8,128)(2,1)S(1)} %get-tuple-element.7.xc, bf16[256,384]{1,0:T(8,128)(2,1)S(1)} %get-tuple-element.8.bm, bf16[2,128,128]{2,1,0:T(8,128)(2,1)S(1)} %get-tuple-element.9.bc), custom_call_target="tpu_custom_call" | custom-call | tf_op jit(solution)/shard_map/pallas_call | solution.py:635

commit v3 on v2

--- a/solution.py
+++ b/solution.py
@@ -41,11 +41,9 @@
 def kernel(tiles, levs, *refs):
     rows, members, cells = refs[2].shape
     group = refs[3].shape[1]
-    whole, coarse, few = rows * (members + 1), rows * group, rows
-    scopes = [
-        pltpu.ACC(mxu)((height, cells), F32)
-        for height in (whole, whole, whole, coarse, few) for mxu in range(2)
-    ]
+    outer, inner = 2 * HB * members + rows, (rows - 2 * HB) * members
+    heights = (outer, inner, outer, inner, outer + inner, outer, rows)
+    scopes = [pltpu.ACC(mxu)((height, cells), F32) for height in heights for mxu in range(2)]
     pl.run_scoped(lambda *sums: body(tiles, levs, sums, *refs), *scopes)
 
 
@@ -61,12 +59,13 @@
     fine = pert_hbm.shape[2]
     span = cells + LANE
     window = rows + 2 * HB
-    edge = HB * members + rows
+    edge = HB * members + 2 * HB
     last = cells - LANE
     comb_at, low_at = HB * members, HB * members + rows
     whole = rows * (members + 1)
     pcomb_at = comb_at // 2
-    pedge = pcomb_at + rows
+    pedge = pcomb_at + 2 * HB
+    pinner_at = rows * members // 2 + 2 * HB
     order = order_of(rows)
     pairs = pairs_of(rows)
     half = HB // 2
@@ -77,7 +76,10 @@
         return place * members + (rows if place >= HB else 0)
 
     assert cells == WIDE * LANE and window * members <= 2 * cells and window * group <= cells
-    ahead, behind, rim_sum, coarse_sum, few_sum = (sums[i : i + 2] for i in range(0, 10, 2))
+    slots = [(sums[i : i + 2], sums[i + 2 : i + 4]) for i in (0, 4)]
+    rim_sum, half_sum, few_sum = (sums[i : i + 2] for i in (8, 10, 12))
+    outer, inner = 2 * HB * members + rows, (rows - 2 * HB) * members
+    assert inner == rows * group
     turns = [0, 0]
 
     def product(into, mxu, left, right, transpose=False):
@@ -86,6 +88,9 @@
         pltpu.matmul_push_rhs(right, staging_register=turn, mxu_index=mxu, transpose=transpose)
         pltpu.matmul_acc_lhs(into[mxu], left, load_staged_rhs=turn)
 
+    def again(into, mxu, left):
+        pltpu.matmul_acc_lhs(into[mxu], left)
+
     t = lax.axis_index("tile")
     v = lax.axis_index("lev")
     first = v * rows
@@ -117,7 +122,7 @@
         when(1, lambda: settle(filler(count), send.at[1]))
         when(-1, lambda: settle(filler(count), send.at[2]))
 
-    own = pl.ds(HB, rows)
+    own = pl.ds(0, rows)
     loads = [
         pltpu.make_async_copy(mc_hbm, mc.at[own], load_sem.at[0]),
         pltpu.make_async_copy(cc_hbm, cc.at[own], load_sem.at[1]),
@@ -137,95 +142,13 @@
 
     barrier = pltpu.get_barrier_semaphore()
     for dt in (-1, 1):
-        pl.when(jnp.logical_not(below[dt]))(lambda dt=dt: signal(barrier, dt, 0))
+        greets = jnp.logical_or(v <= 1, jnp.logical_not(below[dt]))
+        pl.when(greets)(lambda dt=dt: signal(barrier, dt, 0))
     for dt in (-1, 0, 1):
         when(1, lambda dt=dt: signal(barrier, dt, 1))
         pl.when(v == 1)(lambda dt=dt: signal(barrier, dt, -1))
     for load in loads[3:]:
         load.start()
-    lower_tiles = jnp.where(t > 0, 1, 0) + jnp.where(t == tiles - 1, 1, 0)
-    pl.semaphore_wait(barrier, lower_tiles + (3 if levs > 1 else 0))
-    for dt in (-1, 1):
-        pl.when(below[dt])(lambda dt=dt: signal(ready.at[0], dt, 0))
-    for dt in (-1, 0, 1):
-        pl.when(v > 1)(lambda dt=dt: signal(ready.at[1], dt, -1))
-
-    def remote(src, dst, send_at, recv_at, dt, dl):
-        return dl, pltpu.make_async_remote_copy(
-            src_ref=src, dst_ref=dst, send_sem=send_at, recv_sem=recv_at,
-            device_id=(beside[dt], v + dl), device_id_type=MESH,
-        )
-
-    level_src = {1: rows, -1: HB}
-    level_dst = {1: 0, -1: HB + rows}
-    entry_src = {1: len(pairs) - half, -1: 0}
-    tile_row = {1: 0, -1: pcomb_at}
-    lev_row = {1: 0, -1: comb_at}
-    lev1, late, tile1, diag1, tile2, diag2, lev2 = [], [], [], [], [], [], []
-    for dl in (-1, 1):
-        floor = (1 - dl) // 2
-        for buf, copies, at in ((mc, lev1, 0), (cc, lev1, 0), (cp, late, 5)):
-            copies.append(remote(
-                buf.at[pl.ds(level_src[dl], HB)], buf.at[pl.ds(level_dst[dl], HB)],
-                send.at[1 + floor], recv1.at[at + floor], 0, dl))
-        lev2.append(remote(
-            out_own.at[pl.ds(lev_row[dl], edge)], r_lev.at[floor],
-            send.at[1 + floor], recv2.at[floor], 0, dl))
-        for dt in (-1, 1):
-            side = (1 + dt) // 2
-            diag1.append(remote(
-                pk.at[side, pl.ds(entry_src[dl], half), pl.ds(0, members + group)],
-                rd.at[floor, side],
-                send.at[1 + floor], recv1.at[2 + floor], dt, dl))
-            diag2.append(remote(
-                out_rim.at[side, pl.ds(tile_row[dl], pedge)], r_diag.at[floor, side],
-                send.at[1 + floor], recv2.at[2 + floor], dt, dl))
-    for dt in (-1, 1):
-        side = (1 + dt) // 2
-        tile1.append(remote(pk.at[side], rt.at[side], send.at[0], recv1.at[4], dt, 0))
-        tile2.append(remote(out_rim.at[side], r_tile.at[side], send.at[0], recv2.at[4], dt, 0))
-    near = HB * (members + group) * cells
-    extra = HB * group * cells
-
-    @pl.when(v == 0)
-    def _():
-        for buf in (mc, cc, cp):
-            buf[0:HB] = jnp.zeros((HB,) + buf.shape[1:], BF16)
-        rd[0] = jnp.zeros(rd.shape[1:], BF16)
-        r_lev[0] = jnp.zeros(r_lev.shape[1:], BF16)
-        r_diag[0] = jnp.zeros(r_diag.shape[1:], BF16)
-
-    @pl.when(v == levs - 1)
-    def _():
-        for buf in (mc, cc, cp):
-            buf[HB + rows :] = jnp.zeros((HB,) + buf.shape[1:], BF16)
-        rd[1] = jnp.zeros(rd.shape[1:], BF16)
-        r_lev[1] = jnp.zeros(r_lev.shape[1:], BF16)
-        r_diag[1] = jnp.zeros(r_diag.shape[1:], BF16)
-
-    def lower(shape):
-        return lax.broadcasted_iota(jnp.int32, shape, len(shape) - 1) < CW
-
-    def turned(value):
-        return pltpu.roll(value, CW, 1)
-
-    for load in loads[:3]:
-        load.wait()
-    begin([x for x in lev1 if x[0] < 0])
-    start_first([x for x in lev1 if x[0] > 0])
-    for k, (a, b) in enumerate(pairs):
-        for buf, r0, rn in ((mc, 0, members), (cc, members, group), (cp, members + group, group)):
-            low = lower((rn, LANE))
-            near_a, near_b = (buf[HB + i, :, 0:LANE].astype(F32) for i in (a, b))
-            far_a, far_b = (buf[HB + i, :, last:].astype(F32) for i in (a, b))
-            pk[0, k, r0 : r0 + rn, :] = jnp.where(low, near_a, turned(near_b)).astype(BF16)
-            pk[1, k, r0 : r0 + rn, :] = jnp.where(low, turned(far_b), far_a).astype(BF16)
-    begin([x for x in diag1 if x[0] < 0])
-    start_first([x for x in diag1 if x[0] > 0])
-    for dt, (dl, copy) in zip((-1, 1), tile1):
-        pl.when(below[dt])(copy.start)
-    for load in loads[3:6]:
-        load.wait()
     pack = 16
     base_rows = lax.broadcasted_iota(jnp.int32, (pack, LANE), 0).astype(jnp.int16)
 
@@ -247,17 +170,103 @@
         return carry
 
     steps = fine // LANE
-    lax.fori_loop(0, steps // 2, build, 0)
-    pl.when(t < tiles - 1)(lambda: pl.semaphore_wait(ready.at[0], 2 - lower_tiles))
+
+    def build_part(begin_at, end_at):
+        if begin_at == 0:
+            for load in loads[3:6]:
+                load.wait()
+        lax.fori_loop(begin_at, end_at, build, 0)
+
+    pl.when(v == 0)(lambda: build_part(0, steps // 2))
+    lower_tiles = jnp.where(t > 0, 1, 0) + jnp.where(t == tiles - 1, 1, 0)
+    greeting = jnp.where(v <= 1, 2, lower_tiles)
+    pl.semaphore_wait(barrier, greeting + (3 if levs > 1 else 0))
+    for dt in (-1, 1):
+        answers = jnp.logical_and(v > 1, below[dt])
+        pl.when(answers)(lambda dt=dt: signal(ready.at[0], dt, 0))
+    for dt in (-1, 0, 1):
+        pl.when(v > 1)(lambda dt=dt: signal(ready.at[1], dt, -1))
+
+    def remote(src, dst, send_at, recv_at, dt, dl):
+        return dl, pltpu.make_async_remote_copy(
+            src_ref=src, dst_ref=dst, send_sem=send_at, recv_sem=recv_at,
+            device_id=(beside[dt], v + dl), device_id_type=MESH,
+        )
+
+    level_src = {1: rows - HB, -1: 0}
+    level_dst = {1: rows, -1: rows + HB}
+    entry_src = {1: len(pairs) - half, -1: 0}
+    tile_row = {1: 0, -1: pcomb_at}
+    lev_row = {1: 0, -1: comb_at}
+    lev1, late, tile1, diag1, tile2, diag2, lev2 = [], [], [], [], [], [], []
+    for dl in (-1, 1):
+        floor = (1 - dl) // 2
+        for buf, copies, at in ((mc, lev1, 0), (cc, lev1, 0), (cp, late, None)):
+            copies.append(remote(
+                buf.at[pl.ds(level_src[dl], HB)], buf.at[pl.ds(level_dst[dl], HB)],
+                send.at[1 + floor], recv2.at[floor] if at is None else recv1.at[at + floor], 0, dl))
+        lev2.append(remote(
+            out_own.at[pl.ds(lev_row[dl], edge)], r_lev.at[floor],
+            send.at[1 + floor], recv2.at[floor], 0, dl))
+        for dt in (-1, 1):
+            side = (1 + dt) // 2
+            diag1.append(remote(
+                pk.at[side, pl.ds(entry_src[dl], half), pl.ds(0, members + group)],
+                rd.at[floor, side],
+                send.at[1 + floor], recv1.at[2 + floor], dt, dl))
+            diag2.append(remote(
+                out_rim.at[side, pl.ds(tile_row[dl], pedge)], r_diag.at[floor, side],
+                send.at[1 + floor], recv2.at[floor], dt, dl))
+    for dt in (-1, 1):
+        side = (1 + dt) // 2
+        tile1.append(remote(pk.at[side], rt.at[side], send.at[0], recv1.at[4], dt, 0))
+        tile2.append(remote(out_rim.at[side], r_tile.at[side], send.at[0], recv2.at[2], dt, 0))
+    near = HB * (members + group) * cells
+    extra = HB * group * cells
+
+    @pl.when(v == 0)
+    def _():
+        for buf in (mc, cc, cp):
+            buf[rows : rows + HB] = jnp.zeros((HB,) + buf.shape[1:], BF16)
+        rd[0] = jnp.zeros(rd.shape[1:], BF16)
+        r_lev[0] = jnp.zeros(r_lev.shape[1:], BF16)
+        r_diag[0] = jnp.zeros(r_diag.shape[1:], BF16)
+
+    @pl.when(v == levs - 1)
+    def _():
+        for buf in (mc, cc, cp):
+            buf[rows + HB :] = jnp.zeros((HB,) + buf.shape[1:], BF16)
+        rd[1] = jnp.zeros(rd.shape[1:], BF16)
+        r_lev[1] = jnp.zeros(r_lev.shape[1:], BF16)
+        r_diag[1] = jnp.zeros(r_diag.shape[1:], BF16)
+
+    def lower(shape):
+        return lax.broadcasted_iota(jnp.int32, shape, len(shape) - 1) < CW
+
+    def turned(value):
+        return pltpu.roll(value, CW, 1)
+
+    for load in loads[:3]:
+        load.wait()
+    begin([x for x in lev1 if x[0] < 0])
+    start_first([x for x in lev1 if x[0] > 0])
+    for k, (a, b) in enumerate(pairs):
+        for buf, r0, rn in ((mc, 0, members), (cc, members, group), (cp, members + group, group)):
+            low = lower((rn, LANE))
+            near_a, near_b = (buf[i, :, 0:LANE].astype(F32) for i in (a, b))
+            far_a, far_b = (buf[i, :, last:].astype(F32) for i in (a, b))
+            pk[0, k, r0 : r0 + rn, :] = jnp.where(low, near_a, turned(near_b)).astype(BF16)
+            pk[1, k, r0 : r0 + rn, :] = jnp.where(low, turned(far_b), far_a).astype(BF16)
+    begin([x for x in diag1 if x[0] < 0])
+    start_first([x for x in diag1 if x[0] > 0])
     for dt, (dl, copy) in zip((-1, 1), tile1):
-        pl.when(jnp.logical_not(below[dt]))(copy.start)
-    lax.fori_loop(steps // 2, steps, build, 0)
-    inner = jnp.logical_and(v > 0, v < levs - 1)
-    pl.when(inner)(lambda: pl.semaphore_wait(ready.at[1], 3))
-    for dl, copy in lev1 + diag1:
-        if dl > 0:
-            pl.when(inner)(copy.start)
-
+        pl.when(jnp.logical_or(v <= 1, below[dt]))(copy.start)
+    pl.when(v > 0)(lambda: build_part(0, steps // 2))
+    asks = jnp.logical_and(v > 1, t < tiles - 1)
+    pl.when(asks)(lambda: pl.semaphore_wait(ready.at[0], 2 - lower_tiles))
+    for dt, (dl, copy) in zip((-1, 1), tile1):
+        pl.when(jnp.logical_and(v > 1, jnp.logical_not(below[dt])))(copy.start)
+    build_part(steps // 2, steps)
     factors = vert[...].astype(BF16)
     factors = jnp.concatenate(
         [factors, jnp.zeros((total_levels, cells - total_levels), BF16)], axis=1)
@@ -293,7 +302,8 @@
         ]
 
     def natural(seg):
-        return seg - HB
+        halo = jnp.where(seg < rows + HB, seg - rows - HB, seg - HB)
+        return jnp.where(seg < rows, seg, halo)
 
     def stored(seg):
         inner = jnp.where(seg < 2 * HB, seg + rows - 2 * HB, seg - 2 * HB)
@@ -333,27 +343,35 @@
             value = jnp.concatenate([value, jnp.zeros((cells - height, cells), BF16)], axis=0)
         return value
 
-    def localize(members_in, coarse_in, coarse_by, out):
-        wide = members_in.shape[-1]
-        flat = members_in.reshape(window * members, wide)
-        product(ahead, 0, side_by_side(am), square(flat[0:cells]))
-        product(ahead, 1, side_by_side(am, 2), square(flat[cells:]))
-        flat = coarse_in.astype(F32).reshape(window * group, wide).astype(BF16)
-        product(coarse_sum, 1, side_by_side(ac), square(flat))
-        value = pltpu.matmul_pop(ahead[0]) + pltpu.matmul_pop(ahead[1])
-        local = pltpu.matmul_pop(coarse_sum[1])
+    def banded(r0, r1, p0):
+        return jnp.concatenate([am[p0, r0:r1, :], am[p0 + 1, r0:r1, :]], axis=1)
+
+    def flat_of(ref, l0, l1):
+        value = ref[l0:l1]
+        return square(value.reshape((l1 - l0) * members, value.shape[-1]))
+
+    def coarse_product(into, ref):
+        value = ref[...].astype(F32)
+        flat = value.reshape(window * group, value.shape[-1]).astype(BF16)
+        product(into, 1, side_by_side(ac), square(flat))
+
+    def put_outer(value, local, by_ref, out, wide):
         for p in range(wide // LANE):
             lanes = slice(p * LANE, (p + 1) * LANE)
             part = value[:, lanes].astype(BF16)
             out[p, 0:comb_at, :] = part[0:comb_at]
-            out[p, low_at:, :] = part[low_at:]
+            out[p, low_at:outer, :] = part[low_at:]
             mixed = [
-                local[place * group : (place + 1) * group, lanes] * coarse_by[i, :, lanes].astype(F32)
+                local[place * group : (place + 1) * group, lanes] * by_ref[i, :, lanes].astype(F32)
                 for place, i in enumerate(order)
             ]
             sums = [fold(mixed[g : g + 8]) for g in range(0, rows, 8)]
             out[p, comb_at:low_at, :] = jnp.concatenate(sums, axis=0).astype(BF16)
 
+    def put_inner(value, out, wide):
+        for p in range(wide // LANE):
+            out[p, outer:, :] = value[:, p * LANE : (p + 1) * LANE].astype(BF16)
+
     def strip(ref, chunk, r0, r1):
         parts = [ref[chunk * WIDE + i, r0:r1, :] for i in range(WIDE)]
         return jnp.concatenate(parts, axis=1)
@@ -361,44 +379,79 @@
     def summed(value, chunk, part):
         terms = [[] for _ in range(WIDE)]
         for i in order[part * 8 : part * 8 + 8]:
+            at = level_at(i) - (outer if part else 0)
             for piece in range(WIDE):
                 lanes = slice(piece * LANE, (piece + 1) * LANE)
-                at = (chunk * WIDE + piece) * LANE
-                member = pert[i, :, at : at + LANE].astype(F32)
-                product_ = member * value[level_at(i) : level_at(i) + members, lanes]
+                fine_at = (chunk * WIDE + piece) * LANE
+                member = pert[i, :, fine_at : fine_at + LANE].astype(F32)
+                product_ = member * value[at : at + members, lanes]
                 total = product_[0:8]
                 for r in range(8, members, 8):
                     total = total + product_[r : r + 8]
                 terms[piece].append(total)
+        return [fold(term) for term in terms]
+
+    def combined(value, piece, part):
         at = comb_at + part * 8
-        return [
-            fold(terms[piece]) + value[at : at + 8, piece * LANE : (piece + 1) * LANE]
-            for piece in range(WIDE)
-        ]
-
+        return value[at : at + 8, piece * LANE : (piece + 1) * LANE]
+
+    chunks = fine // (WIDE * LANE)
+
+    def slot(chunk):
+        return slots[(chunk // 2) % 2], chunk % 2
+
+    def sweep(start, take, c0, c1):
+        for chunk in range(c0, min(c0 + 4, c1)):
+            start(chunk)
+        for chunk in range(c0, c1):
+            take(chunk, chunk + 4 < c1)
+
+    def begin_inner(chunk):
+        into, mxu = slot(chunk)
+        product(into[1], mxu, side_by_side(fld)[outer:], strip(matrix, chunk, 0, cells))
+
+    def take_inner(chunk, more):
+        into, mxu = slot(chunk)
+        value = pltpu.matmul_pop(into[1][mxu])
+        if more:
+            begin_inner(chunk + 4)
+        for piece, total in enumerate(summed(value, chunk, 1)):
+            line[chunk * WIDE + piece, 8:16, :] = total
+
+    def begin_outer(chunk):
+        into, mxu = slot(chunk)
+        product(into[0], mxu, side_by_side(fld)[0:outer], strip(matrix, chunk, 0, cells))
+
+    def take_outer(chunk, more):
+        into, mxu = slot(chunk)
+        value = pltpu.matmul_pop(into[0][mxu])
+        if more:
+            begin_outer(chunk + 4)
+        for piece, total in enumerate(summed(value, chunk, 0)):
+            n = chunk * WIDE + piece
+            line[n, 0:8, :] = total + combined(value, piece, 0)
+            line[n, 8:16, :] += combined(value, piece, 1)
+
+    inner = jnp.logical_and(v > 0, v < levs - 1)
+    pl.when(inner)(lambda: pl.semaphore_wait(ready.at[1], 3))
+    for dl, copy in lev1 + diag1:
+        if dl > 0:
+            pl.when(inner)(copy.start)
+
+    product(slots[0][1], 0, banded(outer, whole, 0), flat_of(mc, 0, rows))
+    put_inner(pltpu.matmul_pop(slots[0][1][0]), fld, cells)
+    loads[6].wait()
+    sweep(begin_inner, take_inner, 0, chunks)
     when(-1, lambda: settle(filler(near), recv1.at[0]))
     when(1, lambda: settle(filler(near), recv1.at[1]))
     begin(late)
-    localize(mc[...], cc[...], cp[own], fld)
-    loads[6].wait()
-    chunks = fine // (WIDE * LANE)
-
-    def slot(chunk):
-        return (ahead, behind)[(chunk // 2) % 2], chunk % 2
-
-    def first_product(chunk):
-        product(*slot(chunk), side_by_side(fld), strip(matrix, chunk, 0, cells))
-
-    for chunk in range(min(4, chunks)):
-        first_product(chunk)
-    for chunk in range(chunks):
-        into, mxu = slot(chunk)
-        interp = pltpu.matmul_pop(into[mxu])
-        if chunk + 4 < chunks:
-            first_product(chunk + 4)
-        for part in range(rows // 8):
-            for piece, total in enumerate(summed(interp, chunk, part)):
-                line[chunk * WIDE + piece, part * 8 : part * 8 + 8, :] = total
+    (first_outer, first_inner), _ = slots
+    product(first_outer, 0, banded(0, outer, 0), flat_of(mc, 0, rows))
+    product(first_outer, 1, banded(0, outer, 2), flat_of(mc, rows, window))
+    coarse_product(first_inner, cc)
+    value = pltpu.matmul_pop(first_outer[0]) + pltpu.matmul_pop(first_outer[1])
+    put_outer(value, pltpu.matmul_pop(first_inner[1]), cp, fld, cells)
+    sweep(begin_outer, take_outer, 0, chunks)
     def unpack(from_next, from_prev):
         low = lower(from_next.shape)
         nxt, prv = from_next.astype(F32), from_prev.astype(F32)
@@ -408,47 +461,55 @@
         value = value.astype(BF16)
         rim_m[level] = value[0:members]
         rim_c[level] = value[members : members + group]
-        if HB <= level < HB + rows:
-            rim_p[level - HB] = value[members + group :]
+        if level < rows:
+            rim_p[level] = value[members + group :]
 
     settle(rt, recv1.at[4])
     for k, (a, b) in enumerate(pairs):
         va, vb = unpack(rt[0, k], rt[1, k])
-        keep(HB + a, va)
-        keep(HB + b, vb)
+        keep(a, va)
+        keep(b, vb)
+    product(half_sum, 0, banded(0, outer, 0), flat_of(rim_m, 0, rows))
+    again(first_inner, 0, banded(outer, whole, 0))
     when(-1, lambda: settle(rd.at[0], recv1.at[2]))
     when(1, lambda: settle(rd.at[1], recv1.at[3]))
     for floor in range(2):
         for k in range(half):
             va, vb = unpack(rd[floor, 0, k], rd[floor, 1, k])
-            base = floor * (HB + rows)
+            base = rows + floor * HB
             keep(base + k, va)
             keep(base + k + half, vb)
-    localize(rim_m[...], rim_c[...], rim_p[...], fld_rim)
+    product(half_sum, 1, banded(0, outer, 2), flat_of(rim_m, rows, window))
+    coarse_product(first_inner, rim_c)
+    value = pltpu.matmul_pop(half_sum[0]) + pltpu.matmul_pop(half_sum[1])
+    put_inner(pltpu.matmul_pop(first_inner[0]), fld_rim, LANE)
+    put_outer(value, pltpu.matmul_pop(first_inner[1]), rim_p, fld_rim, LANE)
     rim_fields = jnp.concatenate([fld_rim[0], jnp.zeros((whole, cells - LANE), BF16)], axis=1)
     def rim_of(chunk):
         return square(strip(matrix, chunk, cells, span))
 
-    def rim_product(chunk):
-        product(*slot(chunk), rim_fields, rim_of(chunk))
-
-    def own_product(chunk):
-        product(
-            ahead, chunk % 2, strip(adj, chunk, 0, whole), strip(matrix, chunk, 0, cells),
-            transpose=True,
-        )
-
-    for chunk in range(min(4, chunks)):
-        rim_product(chunk)
-    for chunk in range(chunks):
+    def begin_rim(chunk):
         into, mxu = slot(chunk)
-        interp = pltpu.matmul_pop(into[mxu])
-        if chunk + 4 < chunks:
-            rim_product(chunk + 4)
+        product(into[0], mxu, rim_fields[0:outer], rim_of(chunk))
+        again(into[1], mxu, rim_fields[outer:])
+
+    def rim_and_first(chunk):
+        value = [strip(matrix, chunk, cells, span), strip(matrix, chunk, 0, LANE)]
+        return jnp.concatenate(value, axis=0)
+
+    def second_half(chunk):
+        return square(strip(matrix, chunk, LANE, cells))
+
+    def take_rim(chunk, more):
+        into, mxu = slot(chunk)
+        values = [pltpu.matmul_pop(into[part][mxu]) for part in range(2)]
+        if more:
+            begin_rim(chunk + 4)
         totals = [[] for _ in range(WIDE)]
-        for part in range(rows // 8):
-            for piece, total in enumerate(summed(interp, chunk, part)):
+        for part in range(2):
+            for piece, total in enumerate(summed(values[part], chunk, part)):
                 n = chunk * WIDE + piece
+                total = total + combined(values[0], piece, part)
                 total = total + line[n, part * 8 : part * 8 + 8, :]
                 totals[piece].append(total)
                 for r, i in enumerate(order[part * 8 : part * 8 + 8]):
@@ -459,16 +520,21 @@
         for piece in range(WIDE):
             both = jnp.concatenate(totals[piece], axis=0)
             adj[chunk * WIDE + piece, comb_at:low_at, :] = both.astype(BF16)
-        product(rim_sum, mxu, strip(adj, chunk, 0, whole), rim_of(chunk), transpose=True)
-    early = min(4, chunks)
-    for chunk in range(early):
-        own_product(chunk)
+        product(rim_sum, mxu, strip(adj, chunk, 0, whole), rim_and_first(chunk), transpose=True)
+        product(half_sum, mxu, strip(adj, chunk, 0, outer), second_half(chunk), transpose=True)
+
+    sweep(begin_rim, take_rim, 0, chunks)
     back = pltpu.matmul_pop(rim_sum[0]) + pltpu.matmul_pop(rim_sum[1])
     acc_rim[...] = back[:, 0:LANE]
+    acc_own[:, 0:LANE] = back[:, LANE:]
+    back = pltpu.matmul_pop(half_sum[0]) + pltpu.matmul_pop(half_sum[1])
+    acc_own[0:outer, LANE:] = back[:, 0:LANE]
+    out_own[0:edge, :] = acc_own[0:edge, :].astype(BF16)
+    out_own[edge:, :] = acc_own[low_at:outer, :].astype(BF16)
     def packed_at(k):
         place = order.index(pairs[k][0])
         entry = place // HB * half + place % HB
-        return entry * members + (rows if place >= HB else 0)
+        return entry * members + (2 * HB if place >= HB else 0)
 
     low = lower((members, LANE))
     for k, (a, b) in enumerate(pairs):
@@ -478,22 +544,22 @@
         out_rim[1, at, :] = jnp.where(low, value_a, value_b).astype(BF16)
         out_rim[0, at, :] = jnp.where(low, value_b, value_a).astype(BF16)
     for side in range(2):
-        out_rim[side, pcomb_at : pcomb_at + rows, :] = acc_rim[comb_at:low_at, :].astype(BF16)
+        both = acc_rim[comb_at:low_at, :].astype(BF16)
+        out_rim[side, pcomb_at : pcomb_at + 2 * HB, :] = both[0 : 2 * HB]
+        out_rim[side, pinner_at:, :] = both[2 * HB :]
 
     drain(pk, near + extra + 2 * half * (members + group) * LANE)
-    begin(diag2 + tile2)
-    for chunk in range(early, chunks):
-        own_product(chunk)
-    acc_own[...] = pltpu.matmul_pop(ahead[0]) + pltpu.matmul_pop(ahead[1])
-    out_own[...] = acc_own[...].astype(BF16)
-    begin(lev2)
-    when(-1, lambda: settle(filler(extra), recv1.at[5]))
-    when(1, lambda: settle(filler(extra), recv1.at[6]))
-    settle(r_tile, recv2.at[4])
-    for floor, dl in ((0, -1), (1, 1)):
-        when(dl, lambda floor=floor: settle(r_diag.at[floor], recv2.at[2 + floor]))
-    for floor, dl in ((0, -1), (1, 1)):
-        when(dl, lambda floor=floor: settle(r_lev.at[floor], recv2.at[floor]))
+    begin([x for x in diag2 + lev2 if x[0] < 0] + tile2)
+    for chunk in range(chunks):
+        part = strip(adj, chunk, outer, whole)
+        product(first_inner, chunk % 2, part, second_half(chunk), transpose=True)
+    back = pltpu.matmul_pop(first_inner[0]) + pltpu.matmul_pop(first_inner[1])
+    acc_own[outer:, LANE:] = back[:, 0:LANE]
+    begin([x for x in diag2 + lev2 if x[0] > 0])
+    settle(r_tile, recv2.at[2])
+    far = extra + edge * cells + 2 * pedge * LANE
+    when(-1, lambda: settle(filler(far), recv2.at[0]))
+    when(1, lambda: settle(filler(far), recv2.at[1]))
     def zero_but(value, keep_low):
         low = lower(value.shape)
         return jnp.where(low, value, 0.0) if keep_low else jnp.where(low, 0.0, value)
@@ -520,7 +586,7 @@
             base = acc_own[level_at(i) : level_at(i) + members, :]
             put(xm, stored_at(i), members, joined(base, r_tile, at, swap))
     for floor in range(2):
-        p0, o0 = (0, 0) if floor == 0 else (rows, rows)
+        p0 = o0 = 0 if floor == 0 else 2 * HB
         x0 = 0 if floor == 0 else (HB + rows) * members
         for k in range(half):
             at = slice(p0 + k * members, p0 + (k + 1) * members)
@@ -528,17 +594,20 @@
                 i = k + swap * half
                 base = r_lev[floor, o0 + i * members : o0 + (i + 1) * members, :].astype(F32)
                 put(xm, x0 + i * members, members, joined(base, r_diag.at[floor], at, swap))
-    lines = []
-    for floor in (0, 2, 1):
+    lines, own_lines = [], []
+    for floor in (2, 0, 1):
         if floor == 2:
-            parts = joined(acc_own[comb_at:low_at, :], r_tile, slice(pcomb_at, pcomb_at + rows), 0)
-            chosen = [order.index(i) for i in range(rows)]
-        else:
-            o0 = comb_at if floor == 0 else 0
-            p0 = pcomb_at if floor == 0 else 0
-            base = r_lev[floor, o0 : o0 + rows, :].astype(F32)
-            parts = joined(base, r_diag.at[floor], slice(p0, p0 + rows), 0)
-            chosen = range(HB) if floor == 0 else range(HB, 2 * HB)
+            for p0, a0 in ((pcomb_at, comb_at), (pinner_at, comb_at + 2 * HB)):
+                base = acc_own[a0 : a0 + 2 * HB, :]
+                own_lines.append(joined(base, r_tile, slice(p0, p0 + 2 * HB), 0))
+            for i in range(rows):
+                group_at, row = divmod(order.index(i), 2 * HB)
+                lines.append([part[row : row + 1] for part in own_lines[group_at]])
+            continue
+        o0, p0 = (comb_at, pcomb_at) if floor == 0 else (0, 0)
+        base = r_lev[floor, o0 : o0 + 2 * HB, :].astype(F32)
+        parts = joined(base, r_diag.at[floor], slice(p0, p0 + 2 * HB), 0)
+        chosen = range(HB) if floor == 0 else range(HB, 2 * HB)
         lines += [[part[i : i + 1] for part in parts] for i in chosen]
     for level in range(0, window, 2):
         for i in range(cells // LANE):
@@ -578,8 +647,8 @@
         group = coarse_ctrl.shape[1]
         fine = members_pert.shape[2]
         levels, span, lines = rows + 2 * HB, cells + LANE, rows * (members + 1)
-        edge = HB * members + rows
-        pedge = HB * members // 2 + rows
+        edge = HB * members + 2 * HB
+        pedge = HB * members // 2 + 2 * HB
         packed = rows * members // 2 + rows
         hbm = pl.BlockSpec(memory_space=pl.ANY)
         kinds = members + 2 * group
@@ -616,7 +685,7 @@
                 pltpu.VMEM((fine // LANE, lines, LANE), BF16),
                 pltpu.VMEM((fine // LANE, rows, LANE), F32),
                 pltpu.VMEM((lines, LANE), F32),
-                pltpu.VMEM((lines, cells), BF16),
+                pltpu.VMEM((edge + HB * members, cells), BF16),
                 pltpu.VMEM((2, packed, LANE), BF16),
                 pltpu.VMEM((lines, cells), F32),
                 pltpu.VMEM((2, packed, LANE), BF16),
@@ -624,8 +693,8 @@
                 pltpu.VMEM((2, 2, pedge, LANE), BF16),
                 pltpu.SemaphoreType.DMA((7,)),
                 pltpu.SemaphoreType.DMA((3,)),
-                pltpu.SemaphoreType.DMA((7,)),
                 pltpu.SemaphoreType.DMA((5,)),
+                pltpu.SemaphoreType.DMA((3,)),
                 pltpu.SemaphoreType.REGULAR((2,)),
             ],
             compiler_params=pltpu.CompilerParams(

time: 16.4 us -> 16 us (0.976)
  Pallas kernels: 15.6 us -> 15.2 us
    pallas_call x1, Pallas kernels: 14.7 us -> 14.2 us  [step(): pl.pallas_call(functools.partial(kernel, tiles, levs), out_shape=(pltpu.V...]
where the time goes in v3:
time: 16 us; the launch traced here: 15.8 us
  Pallas kernels  15.2 us (95%)
  between operations  0.64 us (4%)
    pallas_call x1, Pallas kernels, step(): pl.pallas_call(functools.partial(kernel, tiles, levs), out_shape=(pltpu.V...  14.2 us
    pallas_call x1, Pallas kernels, step(): pl.pallas_call(finish, out_shape=(jax.ShapeDtypeStruct((rows, members, ce...  0.97 us

profile of v3, /device:TPU:0, one launch (start us, length us, event | category | flops | bytes accessed | tf_op | source)
XLA Modules:
  0.0 15.8 jit_solution(7156496712209275770)
XLA Ops:
  0.6 14.2 %shard_map.86 = (bf16[384,256]{1,0:T(8,128)(2,1)S(1)}, bf16[192,256]{1,0:T(8,128)(2,1)S(1)}, bf16[256,384]{1,0:T(8,128)(2,1)S(1)}, bf16[2,128,128]{2,1,0:T(8,128)(2,1)S(1)}) custom-call(bf16[16,16,4096]{2,1,0:T(8,128)(2,1)} %refs_0_.1, bf16[16,8,256]{2,1,0:T(8,128)(2,1)} %refs_1_.1, bf16[16,16,256]{2,1,0:T(8,128)(2,1)} %refs_2_.1, ...), custom_call_target="tpu_custom_call" | custom-call | tf_op jit(solution)/shard_map/pallas_call | solution.py:656
  14.9 1.0 %shard_map.87 = (f32[16,16,256]{2,1,0:T(8,128)}, f32[16,8,256]{2,1,0:T(8,128)}) custom-call(bf16[384,256]{1,0:T(8,128)(2,1)S(1)} %get-tuple-element.6.xm, bf16[192,256]{1,0:T(8,128)(2,1)S(1)} %get-tuple-element.7.xc, bf16[256,384]{1,0:T(8,128)(2,1)S(1)} %get-tuple-element.8.bm, bf16[2,128,128]{2,1,0:T(8,128)(2,1)S(1)} %get-tuple-element.9.bc), custom_call_target="tpu_custom_call" | custom-call | tf_op jit(solution)/shard_map/pallas_call | solution.py:704

commit v4 on v3

--- a/solution.py
+++ b/solution.py
@@ -125,12 +125,12 @@
     own = pl.ds(0, rows)
     loads = [
         pltpu.make_async_copy(mc_hbm, mc.at[own], load_sem.at[0]),
-        pltpu.make_async_copy(cc_hbm, cc.at[own], load_sem.at[1]),
-        pltpu.make_async_copy(cp_hbm, cp.at[own], load_sem.at[2]),
-        pltpu.make_async_copy(st_hbm, st, load_sem.at[3]),
-        pltpu.make_async_copy(w_hbm, w, load_sem.at[4]),
-        pltpu.make_async_copy(vert_hbm, vert, load_sem.at[5]),
-        pltpu.make_async_copy(pert_hbm, pert, load_sem.at[6]),
+        pltpu.make_async_copy(cc_hbm, cc.at[own], load_sem.at[0]),
+        pltpu.make_async_copy(cp_hbm, cp.at[own], load_sem.at[0]),
+        pltpu.make_async_copy(st_hbm, st, load_sem.at[1]),
+        pltpu.make_async_copy(w_hbm, w, load_sem.at[2]),
+        pltpu.make_async_copy(vert_hbm, vert, load_sem.at[3]),
+        pltpu.make_async_copy(pert_hbm, pert, load_sem.at[4]),
     ]
     for load in loads[:3]:
         load.start()
@@ -177,7 +177,32 @@
                 load.wait()
         lax.fori_loop(begin_at, end_at, build, 0)
 
+    def lower(shape):
+        return lax.broadcasted_iota(jnp.int32, shape, len(shape) - 1) < CW
+
+    def turned(value):
+        return pltpu.roll(value, CW, 1)
+
+    def take_loads():
+        count = rows * (members + 2 * group) * cells
+        settle(pert.at[pl.ds(0, count // (members * fine))], load_sem.at[0])
+
+    def pack_rims():
+        for k, (a, b) in enumerate(pairs):
+            for buf, r0, rn in ((mc, 0, members), (cc, members, group), (cp, members + group, group)):
+                low = lower((rn, LANE))
+                near_a, near_b = (buf[i, :, 0:LANE].astype(F32) for i in (a, b))
+                far_a, far_b = (buf[i, :, last:].astype(F32) for i in (a, b))
+                pk[0, k, r0 : r0 + rn, :] = jnp.where(low, near_a, turned(near_b)).astype(BF16)
+                pk[1, k, r0 : r0 + rn, :] = jnp.where(low, turned(far_b), far_a).astype(BF16)
+
     pl.when(v == 0)(lambda: build_part(0, steps // 2))
+
+    @pl.when(v == 0)
+    def _():
+        take_loads()
+        pack_rims()
+
     lower_tiles = jnp.where(t > 0, 1, 0) + jnp.where(t == tiles - 1, 1, 0)
     greeting = jnp.where(v <= 1, 2, lower_tiles)
     pl.semaphore_wait(barrier, greeting + (3 if levs > 1 else 0))
@@ -240,23 +265,10 @@
         r_lev[1] = jnp.zeros(r_lev.shape[1:], BF16)
         r_diag[1] = jnp.zeros(r_diag.shape[1:], BF16)
 
-    def lower(shape):
-        return lax.broadcasted_iota(jnp.int32, shape, len(shape) - 1) < CW
-
-    def turned(value):
-        return pltpu.roll(value, CW, 1)
-
-    for load in loads[:3]:
-        load.wait()
+    pl.when(v > 0)(take_loads)
     begin([x for x in lev1 if x[0] < 0])
     start_first([x for x in lev1 if x[0] > 0])
-    for k, (a, b) in enumerate(pairs):
-        for buf, r0, rn in ((mc, 0, members), (cc, members, group), (cp, members + group, group)):
-            low = lower((rn, LANE))
-            near_a, near_b = (buf[i, :, 0:LANE].astype(F32) for i in (a, b))
-            far_a, far_b = (buf[i, :, last:].astype(F32) for i in (a, b))
-            pk[0, k, r0 : r0 + rn, :] = jnp.where(low, near_a, turned(near_b)).astype(BF16)
-            pk[1, k, r0 : r0 + rn, :] = jnp.where(low, turned(far_b), far_a).astype(BF16)
+    pl.when(v > 0)(pack_rims)
     begin([x for x in diag1 if x[0] < 0])
     start_first([x for x in diag1 if x[0] > 0])
     for dt, (dl, copy) in zip((-1, 1), tile1):
@@ -621,20 +633,20 @@
 def finish(xm, xc, bm, bc, mo_hbm, co_hbm, mo, co, sem):
     rows, members, cells = mo.shape
     group = co.shape[1]
-    step = rows // 2
-    copies = []
-    for part in range(2):
+    copies, pieces = [], 4
+    step = rows // pieces
+    left = jnp.concatenate([bc[0], bc[1]], axis=1)[:, 0 : xc.shape[0]]
+    value = jnp.dot(left, xc[...], preferred_element_type=F32)
+    co[...] = value.reshape(rows, group, cells)
+    copies.append(pltpu.make_async_copy(co, co_hbm, sem.at[pieces]))
+    copies[-1].start()
+    for part in range(pieces):
         levels = pl.ds(part * step, step)
         at = slice(part * step * members, (part + 1) * step * members)
         value = jnp.dot(bm[at, :], xm[...], preferred_element_type=F32)
         mo[levels] = value.reshape(step, members, cells)
         copies.append(pltpu.make_async_copy(mo.at[levels], mo_hbm.at[levels], sem.at[part]))
         copies[-1].start()
-    left = jnp.concatenate([bc[0], bc[1]], axis=1)[:, 0 : xc.shape[0]]
-    value = jnp.dot(left, xc[...], preferred_element_type=F32)
-    co[...] = value.reshape(rows, group, cells)
-    copies.append(pltpu.make_async_copy(co, co_hbm, sem.at[2]))
-    copies[-1].start()
     for copy in copies:
         copy.wait()
 
@@ -691,7 +703,7 @@
                 pltpu.VMEM((2, packed, LANE), BF16),
                 pltpu.VMEM((2, edge, cells), BF16),
                 pltpu.VMEM((2, 2, pedge, LANE), BF16),
-                pltpu.SemaphoreType.DMA((7,)),
+                pltpu.SemaphoreType.DMA((5,)),
                 pltpu.SemaphoreType.DMA((3,)),
                 pltpu.SemaphoreType.DMA((5,)),
                 pltpu.SemaphoreType.DMA((3,)),
@@ -712,7 +724,7 @@
             scratch_shapes=[
                 pltpu.VMEM((rows, members, cells), F32),
                 pltpu.VMEM((rows, group, cells), F32),
-                pltpu.SemaphoreType.DMA((3,)),
+                pltpu.SemaphoreType.DMA((5,)),
             ],
             compiler_params=pltpu.CompilerParams(vmem_limit_bytes=4 * 1024 * 1024),
         )(*results)

time: 16 us -> 16 us (level)
  no operation moved by 1% of the time
where the time goes in v4:
time: 16 us; the launch traced here: 15.8 us
  Pallas kernels  15.2 us (95%)
  between operations  0.64 us (4%)
    pallas_call x1, Pallas kernels, step(): pl.pallas_call(functools.partial(kernel, tiles, levs), out_shape=(pltpu.V...  14.2 us
    pallas_call x1, Pallas kernels, step(): pl.pallas_call(finish, out_shape=(jax.ShapeDtypeStruct((rows, members, ce...  0.96 us

profile of v4, /device:TPU:0, one launch (start us, length us, event | category | flops | bytes accessed | tf_op | source)
XLA Modules:
  0.0 15.8 jit_solution(7225883245741241239)
XLA Ops:
  0.6 14.2 %shard_map.86 = (bf16[384,256]{1,0:T(8,128)(2,1)S(1)}, bf16[192,256]{1,0:T(8,128)(2,1)S(1)}, bf16[256,384]{1,0:T(8,128)(2,1)S(1)}, bf16[2,128,128]{2,1,0:T(8,128)(2,1)S(1)}) custom-call(bf16[16,16,4096]{2,1,0:T(8,128)(2,1)} %refs_0_.1, bf16[16,8,256]{2,1,0:T(8,128)(2,1)} %refs_1_.1, bf16[16,16,256]{2,1,0:T(8,128)(2,1)} %refs_2_.1, ...), custom_call_target="tpu_custom_call" | custom-call | tf_op jit(solution)/shard_map/pallas_call | solution.py:668
  14.8 1.0 %shard_map.87 = (f32[16,16,256]{2,1,0:T(8,128)}, f32[16,8,256]{2,1,0:T(8,128)}) custom-call(bf16[384,256]{1,0:T(8,128)(2,1)S(1)} %get-tuple-element.6.xm, bf16[192,256]{1,0:T(8,128)(2,1)S(1)} %get-tuple-element.7.xc, bf16[256,384]{1,0:T(8,128)(2,1)S(1)} %get-tuple-element.8.bm, bf16[2,128,128]{2,1,0:T(8,128)(2,1)S(1)} %get-tuple-element.9.bc), custom_call_target="tpu_custom_call" | custom-call | tf_op jit(solution)/shard_map/pallas_call | solution.py:716

commit v5 on v4

--- a/solution.py
+++ b/solution.py
@@ -456,7 +456,6 @@
     sweep(begin_inner, take_inner, 0, chunks)
     when(-1, lambda: settle(filler(near), recv1.at[0]))
     when(1, lambda: settle(filler(near), recv1.at[1]))
-    begin(late)
     (first_outer, first_inner), _ = slots
     product(first_outer, 0, banded(0, outer, 0), flat_of(mc, 0, rows))
     product(first_outer, 1, banded(0, outer, 2), flat_of(mc, rows, window))
@@ -504,6 +503,8 @@
         into, mxu = slot(chunk)
         product(into[0], mxu, rim_fields[0:outer], rim_of(chunk))
         again(into[1], mxu, rim_fields[outer:])
+
+    begin(late)
 
     def rim_and_first(chunk):
         value = [strip(matrix, chunk, cells, span), strip(matrix, chunk, 0, LANE)]

time: 16 us -> 16 us (level)
  no operation moved by 1% of the time
where the time goes in v5:
time: 16 us; the launch traced here: 15.9 us
  Pallas kernels  15.2 us (95%)
  between operations  0.64 us (4%)
    pallas_call x1, Pallas kernels, step(): pl.pallas_call(functools.partial(kernel, tiles, levs), out_shape=(pltpu.V...  14.3 us
    pallas_call x1, Pallas kernels, step(): pl.pallas_call(finish, out_shape=(jax.ShapeDtypeStruct((rows, members, ce...  0.96 us

profile of v5, /device:TPU:0, one launch (start us, length us, event | category | flops | bytes accessed | tf_op | source)
XLA Modules:
  0.0 15.9 jit_solution(12494416440751189410)
XLA Ops:
  0.6 14.3 %shard_map.86 = (bf16[384,256]{1,0:T(8,128)(2,1)S(1)}, bf16[192,256]{1,0:T(8,128)(2,1)S(1)}, bf16[256,384]{1,0:T(8,128)(2,1)S(1)}, bf16[2,128,128]{2,1,0:T(8,128)(2,1)S(1)}) custom-call(bf16[16,16,4096]{2,1,0:T(8,128)(2,1)} %refs_0_.1, bf16[16,8,256]{2,1,0:T(8,128)(2,1)} %refs_1_.1, bf16[16,16,256]{2,1,0:T(8,128)(2,1)} %refs_2_.1, ...), custom_call_target="tpu_custom_call" | custom-call | tf_op jit(solution)/shard_map/pallas_call | solution.py:669
  14.9 1.0 %shard_map.87 = (f32[16,16,256]{2,1,0:T(8,128)}, f32[16,8,256]{2,1,0:T(8,128)}) custom-call(bf16[384,256]{1,0:T(8,128)(2,1)S(1)} %get-tuple-element.6.xm, bf16[192,256]{1,0:T(8,128)(2,1)S(1)} %get-tuple-element.7.xc, bf16[256,384]{1,0:T(8,128)(2,1)S(1)} %get-tuple-element.8.bm, bf16[2,128,128]{2,1,0:T(8,128)(2,1)S(1)} %get-tuple-element.9.bc), custom_call_target="tpu_custom_call" | custom-call | tf_op jit(solution)/shard_map/pallas_call | solution.py:717
